TPU v7x, 16 devices: a whole 2x2x2 slice. The times are simulated.
16 devices in a mesh: tp: 2 (over z), cp: 8 (over y, x, core).
Axes of the slice: x: 2, y: 2, z: 2, core: 2. Of those that a mesh axis runs over, the one named last changes fastest.
Arguments:
- x_in: bfloat16 [8192, 1536], P('cp')
- positions: int32 [8192], P('cp')
- attn_gain: bfloat16 [2, 1536], replicated
- mlp_gain: bfloat16 [2, 1536], replicated
- w_query: bfloat16 [2, 1536, 1536], P(None, None, 'tp')
- b_query: bfloat16 [2, 1536], P(None, 'tp')
- w_key: bfloat16 [2, 1536, 256], P(None, None, 'tp')
- b_key: bfloat16 [2, 256], P(None, 'tp')
- w_value: bfloat16 [2, 1536, 256], P(None, None, 'tp')
- b_value: bfloat16 [2, 256], P(None, 'tp')
- w_out: bfloat16 [2, 1536, 1536], P(None, 'tp')
- w_gate: bfloat16 [2, 1536, 8960], P(None, None, 'tp')
- w_up: bfloat16 [2, 1536, 8960], P(None, None, 'tp')
- w_down: bfloat16 [2, 8960, 1536], P(None, 'tp')
Outputs:
- output 1: bfloat16 [8192, 1536], P('cp')
- output 2: bfloat16 [8192, 2, 128], P('cp', 'tp')
- output 3: bfloat16 [8192, 2, 128], P('cp', 'tp')
- output 4: bfloat16 [8192, 2, 128], P('cp', 'tp')
- output 5: bfloat16 [8192, 2, 128], P('cp', 'tp')
All inputs are finite; a program needn't handle non-finite values.
Results may differ from a plain program's by a relative error of at most 0.02.
Values are sent between devices in bfloat16 or wider.
A program may use at most 1 GiB of HBM per device.

v0:
```python
import functools

import jax
import jax.numpy as jnp
from jax import lax
from jax.experimental import pallas as pl
from jax.experimental.pallas import tpu as pltpu
from jax.sharding import PartitionSpec as P

HEAD_DIM = 128
WINDOW = 4096
SCORE_SCALE = (HEAD_DIM ** -0.5) * 1.4426950408889634
MIB = 1024 * 1024
MESH = pl.DeviceIdType.MESH


def rms_rows(hidden_f, gain_f):
    variance = jnp.mean(hidden_f * hidden_f, axis=-1, keepdims=True)
    return (hidden_f * lax.rsqrt(variance + 1e-6) * gain_f).astype(jnp.bfloat16)


def qkv_kernel(x_ref, gain_ref, wq_ref, wk_ref, wv_ref, bq_ref, bk_ref, bv_ref, cos_ref, sin_ref, q_ref, k_ref, v_ref, kv_ref):
    normed = rms_rows(x_ref[...].astype(jnp.float32), gain_ref[...].astype(jnp.float32))
    cos_tab = cos_ref[...]
    sin_tab = sin_ref[...]

    def rope(block):
        return (block * cos_tab + pltpu.roll(block, HEAD_DIM // 2, 1) * sin_tab).astype(jnp.bfloat16)

    k_f = jnp.dot(normed, wk_ref[...], preferred_element_type=jnp.float32) + bk_ref[...].astype(jnp.float32)
    k_b = rope(k_f)
    k_ref[...] = k_b
    kv_ref[:, :HEAD_DIM] = k_b
    v_f = jnp.dot(normed, wv_ref[...], preferred_element_type=jnp.float32) + bv_ref[...].astype(jnp.float32)
    v_b = v_f.astype(jnp.bfloat16)
    v_ref[...] = v_b
    kv_ref[:, HEAD_DIM:] = v_b
    q_f = jnp.dot(normed, wq_ref[...], preferred_element_type=jnp.float32) + bq_ref[...].astype(jnp.float32)
    for head in range(q_ref.shape[1] // HEAD_DIM):
        cols = slice(head * HEAD_DIM, (head + 1) * HEAD_DIM)
        q_ref[:, cols] = rope(q_f[:, cols])


def qkv(layer, x, gain, wq, wk, wv, bq, bk, bv, cos_tab, sin_tab):
    rows, width = x.shape
    q_cols = wq.shape[2]
    block = min(rows, 256)

    def whole(w):
        return pl.BlockSpec((None,) + w.shape[1:], lambda i: (layer, 0, 0))

    def table():
        return pl.BlockSpec((block, HEAD_DIM), lambda i: (i, 0))

    def out(cols):
        return pl.BlockSpec((block, cols), lambda i: (i, 0))

    return pl.pallas_call(
        qkv_kernel,
        grid=(rows // block,),
        in_specs=[out(width)] + [whole(w) for w in (gain, wq, wk, wv, bq, bk, bv)] + [table(), table()],
        out_specs=[out(c) for c in (q_cols, HEAD_DIM, HEAD_DIM, 2 * HEAD_DIM)],
        out_shape=[jax.ShapeDtypeStruct((rows, c), jnp.bfloat16) for c in (q_cols, HEAD_DIM, HEAD_DIM, 2 * HEAD_DIM)],
        compiler_params=pltpu.CompilerParams(vmem_limit_bytes=32 * MIB),
        cost_estimate=pl.CostEstimate(flops=2 * rows * width * (q_cols + 256), bytes_accessed=rows * width * 4 + width * 2048, transcendentals=0),
        name="qkv",
    )(x, gain, wq, wk, wv, bq, bk, bv, cos_tab, sin_tab)


def attn_kernel(*refs, bq, window_blocks, with_w):
    refs = list(refs)
    q_ref, kv_ref = refs[:2]; refs = refs[2:]
    w_out = refs.pop(0) if with_w else None
    o_ref, o_peer = refs[:2]; refs = refs[2:]
    w_peer = refs.pop(0) if with_w else None
    kv_buf, m_sc, l_sc, acc_sc, send_sems, recv_sems, o_send, o_recv, w_send, w_recv = refs
    rows = q_ref.shape[0]
    heads = q_ref.shape[1] // HEAD_DIM
    cp = lax.axis_index("cp")
    core, xpos, ypos = lax.rem(cp, 2), lax.rem(lax.div(cp, 2), 2), lax.div(cp, 4)
    to_mate, to_x, to_y = 1 - 2 * core, 2 - 4 * xpos, 4 - 8 * ypos
    mate, xnb, ynb, diag = cp + to_mate, cp + to_x, cp + to_y, cp + to_x + to_y
    half = rows // 2

    peer = 1 - lax.axis_index("tp")
    at_cp = lambda i: {"cp": i}
    whole = pl.ds(0, rows)

    def kv_copy(i, src, slot, part, dev):
        return pltpu.make_async_remote_copy(src_ref=src, dst_ref=kv_buf.at[slot, part], send_sem=send_sems.at[i], recv_sem=recv_sems.at[i], device_id=at_cp(dev), device_id_type=MESH)

    first, last = pl.ds(0, half), pl.ds(half, half)
    kv_copies = [
        kv_copy(0, kv_ref, cp, whole, mate),
        kv_copy(1, kv_ref, cp, whole, xnb),
        kv_copy(2, kv_ref, cp, whole, ynb),
        kv_copy(3, kv_buf.at[xnb], xnb, whole, mate),
        kv_copy(4, kv_buf.at[ynb], ynb, whole, mate),
        kv_copy(5, kv_buf.at[xnb, first], xnb, first, ynb),
        kv_copy(6, kv_buf.at[ynb, last], ynb, last, xnb),
        kv_copy(7, kv_buf.at[diag], diag, whole, mate),
    ]
    if with_w:
        quarter = w_out.shape[1] // 2
        mine = pl.ds(pl.multiple_of(core * quarter, quarter), quarter)
        w_z = pltpu.make_async_remote_copy(src_ref=w_out.at[:, mine], dst_ref=w_peer.at[:, mine], send_sem=w_send.at[0], recv_sem=w_recv.at[0], device_id={"tp": peer}, device_id_type=MESH)
        w_d = pltpu.make_async_remote_copy(src_ref=w_peer.at[:, mine], dst_ref=w_peer.at[:, mine], send_sem=w_send.at[1], recv_sem=w_recv.at[1], device_id=at_cp(mate), device_id_type=MESH)

    barrier = pltpu.get_barrier_semaphore()
    for dev in (at_cp(mate), at_cp(xnb), at_cp(ynb), {"tp": peer}):
        pl.semaphore_signal(barrier, inc=1, device_id=dev, device_id_type=MESH)
    pl.semaphore_wait(barrier, 4)
    for copy in kv_copies[:3]:
        copy.start()
    if with_w:
        w_z.start()

    def o_copy(qb):
        part = pl.ds(pl.multiple_of(qb * bq, bq), bq)
        return pltpu.make_async_remote_copy(src_ref=o_ref.at[part], dst_ref=o_peer.at[part], send_sem=o_send.at[qb], recv_sem=o_recv.at[qb], device_id={"tp": peer}, device_id_type=MESH)

    def block(q0, kb, vb, keep):
        bk = kb.shape[0]

        def scores(h):
            qh = q_ref[pl.ds(q0, bq), h * HEAD_DIM:(h + 1) * HEAD_DIM]
            return lax.dot_general(qh, kb, (((1,), (1,)), ((), ())), preferred_element_type=jnp.float32)

        def soft(h, s):
            if keep is not None:
                s = jnp.where(keep, s, -1e30)
            m_old = m_sc[h]
            m_new = jnp.maximum(m_old, jnp.max(s, axis=1, keepdims=True) * SCORE_SCALE)
            m_sc[h] = m_new
            alpha = jnp.exp2(m_old - m_new)
            p = jnp.exp2(s * SCORE_SCALE - jnp.tile(m_new, (1, bk // HEAD_DIM)))
            if keep is not None:
                p = jnp.where(keep, p, 0.0)
            parts = [p[:, j:j + HEAD_DIM] for j in range(0, bk, HEAD_DIM)]
            while len(parts) > 1:
                parts = [parts[i] + parts[i + 1] for i in range(0, len(parts), 2)]
            l_sc[h] = l_sc[h] * alpha + parts[0]
            return p.astype(jnp.bfloat16), alpha

        def weigh(h, p, alpha):
            acc_sc[h] = acc_sc[h] * alpha + jnp.dot(p, vb, preferred_element_type=jnp.float32)

        s_of, p_of = {}, {}
        for i in range(heads + 2):
            if i < heads:
                s_of[i] = scores(i)
            if i >= 2:
                weigh(i - 2, *p_of.pop(i - 2))
            if 1 <= i <= heads:
                p_of[i - 1] = soft(i - 1, s_of.pop(i - 1))

    def split(ref, *at):
        return ref[at + (slice(None, HEAD_DIM),)], ref[at + (slice(HEAD_DIM, None),)]

    def q_block(qb, carry):
        q0 = pl.multiple_of(qb * bq, bq)
        m_sc[...] = jnp.full(m_sc.shape, -1e30, jnp.float32)
        l_sc[...] = jnp.zeros(l_sc.shape, jnp.float32)
        acc_sc[...] = jnp.zeros(acc_sc.shape, jnp.float32)
        row = lax.broadcasted_iota(jnp.int32, (bq, bq), 0)
        col = lax.broadcasted_iota(jnp.int32, (bq, bq), 1)

        def own_part(j, c):
            block(q0, *split(kv_ref, pl.ds(pl.multiple_of(j * bq, bq), bq)), None)
            return c

        block(q0, *split(kv_ref, pl.ds(q0, bq)), col <= row)
        lax.fori_loop(0, qb, own_part, 0)

        def step_body(step, c):
            src = cp + lax.rem(step, 2) * to_mate + lax.rem(lax.div(step, 2), 2) * to_x + lax.div(step, 4) * to_y
            @pl.when(qb == 0)
            def _():
                @pl.when(step == 1)
                def _():
                    kv_copies[0].wait_recv()

                @pl.when(step == 2)
                def _():
                    kv_copies[1].wait_recv()
                    kv_copies[3].start()
                    kv_copies[5].start()
                    kv_copies[2].wait_recv()
                    kv_copies[4].start()
                    kv_copies[6].start()

                @pl.when(step == 3)
                def _():
                    kv_copies[3].wait_recv()

                @pl.when(step == 5)
                def _():
                    kv_copies[4].wait_recv()

                @pl.when(step == 6)
                def _():
                    kv_copies[5].wait_recv()
                    kv_copies[6].wait_recv()
                    kv_copies[7].start()

                @pl.when(step == 7)
                def _():
                    kv_copies[7].wait_recv()
            @pl.when((src < cp) & (src > cp - window_blocks))
            def _():
                block(q0, *split(kv_buf, src, slice(None)), None)

            if window_blocks < 8:
                @pl.when(src == cp - window_blocks)
                def _():
                    block(q0, *split(kv_buf, src, pl.ds(q0, bq)), col > row)

                    def edge_part(j, cc):
                        block(q0, *split(kv_buf, src, pl.ds(pl.multiple_of(j * bq, bq), bq)), None)
                        return cc

                    lax.fori_loop(qb + 1, rows // bq, edge_part, 0)
            return c

        lax.fori_loop(1, 8, step_body, 0)
        for h in range(heads):
            total = jnp.sum(l_sc[h], axis=1, keepdims=True)
            o_ref[pl.ds(q0, bq), h * HEAD_DIM:(h + 1) * HEAD_DIM] = (acc_sc[h] / total).astype(jnp.bfloat16)
        o_copy(qb).start()
        if with_w:
            @pl.when(qb == 0)
            def _():
                w_z.wait_recv()
                w_d.start()
        return carry

    lax.fori_loop(0, rows // bq, q_block, 0)
    for copy in kv_copies:
        copy.wait_send()
    if with_w:
        w_z.wait_send()
        w_d.wait()
    for qb in range(rows // bq):
        o_copy(qb).wait()

def attention(q, kv, w_out, window_blocks, bq, cid):
    rows, cols = q.shape
    heads = cols // HEAD_DIM
    with_w = w_out is not None
    bf = jnp.bfloat16
    vm = pl.BlockSpec(memory_space=pltpu.VMEM)
    anys = pl.BlockSpec(memory_space=pl.ANY)
    nq = rows // bq
    outs = [jax.ShapeDtypeStruct((rows, cols), bf), jax.ShapeDtypeStruct((rows, cols), bf)]
    if with_w: outs.append(jax.ShapeDtypeStruct(w_out.shape, bf))
    dma = pltpu.SemaphoreType.DMA
    return pl.pallas_call(
        functools.partial(attn_kernel, bq=bq, window_blocks=window_blocks, with_w=with_w),
        in_specs=[vm, vm] + [anys] * with_w,
        out_specs=[vm, anys] + [anys] * with_w,
        out_shape=outs,
        scratch_shapes=[pltpu.VMEM((8, rows, 2 * HEAD_DIM), bf)] + [pltpu.VMEM((heads, bq, HEAD_DIM), jnp.float32)] * 3
        + [dma((8,)), dma((8,)), dma((nq,)), dma((nq,)), dma((2,)), dma((2,))],
        compiler_params=pltpu.CompilerParams(vmem_limit_bytes=48 * MIB, collective_id=cid, has_side_effects=True),
        cost_estimate=pl.CostEstimate(flops=16 * rows * rows * cols, bytes_accessed=rows * cols * 6, transcendentals=0),
        name="attn",
    )(q, kv, *([w_out] if with_w else []))


def out_kernel(place_ref, o_own_ref, o_peer_ref, x_ref, gain_ref, w_own_hbm, w_peer_hbm, x1_ref, h2_ref, w_full, o_full, sems, *, layer):
    half = o_own_ref.shape[1]
    own0 = pl.multiple_of(place_ref[0] * half, half)
    peer0 = pl.multiple_of((1 - place_ref[0]) * half, half)

    @pl.when(pl.program_id(0) == 0)
    def _():
        copies = [
            pltpu.make_async_copy(w_own_hbm.at[layer], w_full.at[pl.ds(own0, half)], sems.at[0]),
            pltpu.make_async_copy(w_peer_hbm.at[layer], w_full.at[pl.ds(peer0, half)], sems.at[1]),
        ]
        for copy in copies:
            copy.start()
        for copy in copies:
            copy.wait()

    o_full[:, pl.ds(own0, half)] = o_own_ref[...]
    o_full[:, pl.ds(peer0, half)] = o_peer_ref[...]
    prod = jnp.dot(o_full[...], w_full[...], preferred_element_type=jnp.float32)
    x1 = (x_ref[...].astype(jnp.float32) + prod).astype(jnp.bfloat16)
    x1_ref[...] = x1
    h2_ref[...] = rms_rows(x1.astype(jnp.float32), gain_ref[...].astype(jnp.float32))


def out_project(layer, place, o_own, o_peer, x, gain, w_own, w_peer):
    rows, half = o_own.shape
    width = x.shape[1]
    block = min(rows, 256)

    def rowspec(cols):
        return pl.BlockSpec((block, cols), lambda i, s: (i, 0))

    return pl.pallas_call(
        functools.partial(out_kernel, layer=layer),
        grid_spec=pltpu.PrefetchScalarGridSpec(
            num_scalar_prefetch=1,
            grid=(rows // block,),
            in_specs=[
                rowspec(half), rowspec(half), rowspec(width),
                pl.BlockSpec((None, 1, width), lambda i, s: (layer, 0, 0)),
                pl.BlockSpec(memory_space=pl.ANY), pl.BlockSpec(memory_space=pl.ANY),
            ],
            out_specs=[rowspec(width), rowspec(width)],
            scratch_shapes=[pltpu.VMEM((2 * half, width), jnp.bfloat16), pltpu.VMEM((block, 2 * half), jnp.bfloat16), pltpu.SemaphoreType.DMA((2,))],
        ),
        out_shape=[jax.ShapeDtypeStruct((rows, width), jnp.bfloat16)] * 2,
        compiler_params=pltpu.CompilerParams(vmem_limit_bytes=32 * MIB),
        cost_estimate=pl.CostEstimate(flops=4 * rows * half * width, bytes_accessed=rows * width * 10 + 4 * half * width, transcendentals=0),
        name="outproj",
    )(place, o_own, o_peer, x, gain, w_own, w_peer)


def mlp_kernel(h_ref, x1_hbm, wg_hbm, wu_hbm, wd_hbm, out_hbm, wg, wu, wd, send, recv, x1_buf, acc, w_sems, send_sems, recv_sems, x_sem, out_sems, *, layer, tiles, chunks):
    peer = 1 - lax.axis_index("tp")
    offs = [sum(tiles[:i]) for i in range(len(tiles))]
    starts = [sum(chunks[:i]) for i in range(len(chunks))]

    def w_copies(i):
        c = pl.ds(offs[i], tiles[i])
        return (
            pltpu.make_async_copy(wg_hbm.at[layer, :, c], wg.at[:, c], w_sems.at[i, 0]),
            pltpu.make_async_copy(wu_hbm.at[layer, :, c], wu.at[:, c], w_sems.at[i, 1]),
            pltpu.make_async_copy(wd_hbm.at[layer, c], wd.at[c], w_sems.at[i, 2]),
        )

    for i in range(len(tiles)):
        for copy in w_copies(i):
            copy.start()
    x_copy = pltpu.make_async_copy(x1_hbm, x1_buf, x_sem.at[0])
    x_copy.start()
    barrier = pltpu.get_barrier_semaphore()
    pl.semaphore_signal(barrier, inc=1, device_id={"tp": peer}, device_id_type=MESH)
    pl.semaphore_wait(barrier, 1)

    swaps = []
    for ci, n in enumerate(chunks):
        r = pl.ds(starts[ci], n)
        for i, t in enumerate(tiles):
            if ci == 0:
                for copy in w_copies(i):
                    copy.wait()
            c = pl.ds(offs[i], t)
            normed = h_ref[r, :]
            gate = jnp.dot(normed, wg[:, c], preferred_element_type=jnp.float32)
            up = jnp.dot(normed, wu[:, c], preferred_element_type=jnp.float32)
            act = (gate * jax.nn.sigmoid(gate) * up).astype(jnp.bfloat16)
            part = jnp.dot(act, wd[c, :], preferred_element_type=jnp.float32)
            if i == 0:
                acc[:n, :] = part
            elif i < len(tiles) - 1:
                acc[:n, :] += part
            else:
                send[r, :] = (acc[:n, :] + part).astype(jnp.bfloat16)
        swap = pltpu.make_async_remote_copy(src_ref=send.at[r], dst_ref=recv.at[r], send_sem=send_sems.at[ci], recv_sem=recv_sems.at[ci], device_id={"tp": peer}, device_id_type=MESH)
        swap.start()
        swaps.append(swap)

    x_copy.wait()
    out_copies = []
    for ci, n in enumerate(chunks):
        r = pl.ds(starts[ci], n)
        swaps[ci].wait()
        total = send[r, :].astype(jnp.float32) + recv[r, :].astype(jnp.float32)
        x1_buf[r, :] = (x1_buf[r, :].astype(jnp.float32) + total).astype(jnp.bfloat16)
        out_copy = pltpu.make_async_copy(x1_buf.at[r], out_hbm.at[r], out_sems.at[ci])
        out_copy.start()
        out_copies.append(out_copy)
    for out_copy in out_copies:
        out_copy.wait()


def mlp(layer, h2, x1, wg, wu, wd, cid):
    rows, width = h2.shape
    cols = wg.shape[2]
    tiles = (256, 512, 768, 1024, 1024, 896)
    chunks = (256,) * (rows // 256)
    nt, nc = len(tiles), len(chunks)
    anys = pl.BlockSpec(memory_space=pl.ANY)
    bf = jnp.bfloat16
    dma = pltpu.SemaphoreType.DMA
    return pl.pallas_call(
        functools.partial(mlp_kernel, layer=layer, tiles=tiles, chunks=chunks),
        in_specs=[pl.BlockSpec(memory_space=pltpu.VMEM), anys, anys, anys, anys],
        out_specs=anys,
        out_shape=jax.ShapeDtypeStruct((rows, width), bf),
        scratch_shapes=[
            pltpu.VMEM((width, cols), bf), pltpu.VMEM((width, cols), bf), pltpu.VMEM((cols, width), bf),
            pltpu.VMEM((rows, width), bf), pltpu.VMEM((rows, width), bf), pltpu.VMEM((rows, width), bf),
            pltpu.VMEM((max(chunks), width), jnp.float32),
            dma((nt, 3)), dma((nc,)), dma((nc,)), dma((1,)), dma((nc,)),
        ],
        compiler_params=pltpu.CompilerParams(vmem_limit_bytes=67043328, collective_id=cid, has_side_effects=True),
        cost_estimate=pl.CostEstimate(flops=6 * rows * width * cols, bytes_accessed=6 * width * cols, transcendentals=0),
        name="mlp",
    )(h2, x1, wg, wu, wd)


def solution(mesh):
    cp_size = mesh.shape["cp"]

    def local_step(x_in, positions, attn_gain, mlp_gain, w_query, b_query, w_key, b_key, w_value, b_value, w_out, w_gate, w_up, w_down):
        block_dev = x_in.shape[0]
        tp = lax.axis_index("tp")
        inv_freq = 1.0 / (1000000.0 ** (jnp.arange(0, HEAD_DIM, 2, dtype=jnp.float32) / HEAD_DIM))
        angles = positions.astype(jnp.float32)[:, None] * inv_freq[None, :]
        cos_half, sin_half = jnp.cos(angles), jnp.sin(angles)
        cos_tab = jnp.concatenate([cos_half, cos_half], axis=1)
        sin_tab = jnp.concatenate([-sin_half, sin_half], axis=1)
        row = lambda a: a[:, None, :]
        attn_gain, mlp_gain, b_query, b_key, b_value = (row(a) for a in (attn_gain, mlp_gain, b_query, b_key, b_value))

        place = jnp.reshape(tp, (1,)).astype(jnp.int32)
        hidden, w_peer, caches = x_in, None, []
        for layer, window_blocks in ((0, cp_size), (1, WINDOW // block_dev)):
            q, k, v, kv = qkv(layer, hidden, attn_gain, w_query, w_key, w_value, b_query, b_key, b_value, cos_tab, sin_tab)
            o, o_peer, *rest = attention(q, kv, w_out if layer == 0 else None, window_blocks, 512, 2 * layer)
            if layer == 0:
                w_peer = rest[0]
            x1, h2 = out_project(layer, place, o, o_peer, hidden, mlp_gain, w_out, w_peer)
            hidden = mlp(layer, h2, x1, w_gate, w_up, w_down, 2 * layer + 1)
            caches.append(k[:, None, :])
            caches.append(v[:, None, :])
        return hidden, caches[0], caches[1], caches[2], caches[3]

    weight_col = P(None, None, "tp")
    bias_col = P(None, "tp")
    weight_row = P(None, "tp", None)
    replicated = P(None, None)
    cache_spec = P("cp", "tp", None)
    in_specs = (P("cp", None), P("cp"), replicated, replicated, weight_col, bias_col, weight_col, bias_col, weight_col, bias_col, weight_row, weight_col, weight_col, weight_row)
    out_specs = (P("cp", None), cache_spec, cache_spec, cache_spec, cache_spec)
    return jax.shard_map(local_step, mesh=mesh, in_specs=in_specs, out_specs=out_specs, check_vma=False)
```

profile of v0, /device:TPU:4, one launch (start us, length us, event | category | flops | bytes accessed | tf_op | source)
XLA Modules:
  0.0 411.3 jit_solution(12034984208012903190)
XLA Ops:
  5.3 1.9 fusion
  7.6 2.7 copy-done.10
  10.3 1.1 copy-done.15
  11.4 6.8 %qkv.2 = (bf16[1024,768]{1,0:T(8,128)(2,1)S(1)}, bf16[1024,128]{1,0:T(8,128)(2,1)}, bf16[1024,128]{1,0:T(8,128)(2,1)}, bf16[1024,256]{1,0:T(8,128)(2,1)S(1)}) custom-call(bf16[1024,1536]{1,0:T(8,128)(2,1)S(1)} %copy-done.12, bf16[2,1,1536]{2,1,0:T(2,128)(2,1)S(1)} %copy.19.gain_ref, bf16[2,1536,768]{2,1,0:T(8,128)(2,1)S(1)} %copy-done.10, ...), custom_call_target="tpu_custom_call" | custom-call | flops 3221225472 | bytes 9437184 | tf_op jit(solution)/shard_map/qkv/pallas_call | solution.py:58
  18.3 94.5 %attn.2 = (bf16[1024,768]{1,0:T(8,128)(2,1)S(1)}, bf16[1024,768]{1,0:T(8,128)(2,1)S(1)}, bf16[2,768,1536]{2,1,0:T(8,128)(2,1)}) custom-call(bf16[1024,768]{1,0:T(8,128)(2,1)S(1)} %get-tuple-element.22.refs_0_, bf16[1024,256]{1,0:T(8,128)(2,1)S(1)} %get-tuple-element.23.refs_1_, bf16[2,768,1536]{2,1,0:T(8,128)(2,1)} %w_own_hbm.3), custom_call_target="tpu_custom_call" | custom-call | flops 12884901888 | bytes 4718592 | tf_op jit(solution)/shard_map/attn/pallas_call | solution.py:257
  112.9 2.3 copy-done.23
  115.2 7.3 %outproj.2 = (bf16[1024,1536]{1,0:T(8,128)(2,1)S(1)}, bf16[1024,1536]{1,0:T(8,128)(2,1)S(1)}) custom-call(s32[1]{0:T(128)} %bitcast.place_ref, bf16[1024,768]{1,0:T(8,128)(2,1)S(1)} %get-tuple-element.24.o_own_ref, bf16[1024,768]{1,0:T(8,128)(2,1)S(1)} %get-tuple-element.25.o_peer_ref, bf16[1024,1536]{1,0:T(8,128)(2,1)S(1)} %copy-done.12, ...), custom_call_target="tpu_custom_call" | custom-call | flops 4831838208 | bytes 20447232 | tf_op jit(solution)/shard_map/outproj/pallas_call | solution.py:302
  122.5 1.7 copy-done.27
  124.2 1.7 copy-done.28
  125.9 89.3 %mlp.2.x_ref = bf16[1024,1536]{1,0:T(8,128)(2,1)} custom-call(bf16[1024,1536]{1,0:T(8,128)(2,1)} %copy-done.28, bf16[1024,1536]{1,0:T(8,128)(2,1)} %copy-done.27, bf16[2,1536,4480]{2,1,0:T(8,128)(2,1)} %wg_hbm.3, bf16[2,1536,4480]{2,1,0:T(8,128)(2,1)} %wu_hbm.3, bf16[2,4480,1536]{2,1,0:T(8,128)(2,1)} %wd_hbm.3), custom_call_target="tpu_custom_call" | custom-call | flops 42278584320 | bytes 41287680 | tf_op jit(solution)/shard_map/mlp/pallas_call | solution.py:390
  215.3 1.0 copy-done.1
  216.3 1.0 copy-done.3
  218.7 2.3 copy-done.11
  221.1 1.1 copy-done.14
  222.2 1.1 copy-done.16
  224.6 1.9 copy-done.21
  226.5 6.1 %qkv.3 = (bf16[1024,768]{1,0:T(8,128)(2,1)S(1)}, bf16[1024,128]{1,0:T(8,128)(2,1)}, bf16[1024,128]{1,0:T(8,128)(2,1)}, bf16[1024,256]{1,0:T(8,128)(2,1)S(1)}) custom-call(bf16[1024,1536]{1,0:T(8,128)(2,1)S(1)} %copy-done.21, bf16[2,1,1536]{2,1,0:T(2,128)(2,1)S(1)} %copy-done.7, bf16[2,1536,768]{2,1,0:T(8,128)(2,1)S(1)} %copy-done.11, ...), custom_call_target="tpu_custom_call" | custom-call | flops 3221225472 | bytes 9437184 | tf_op jit(solution)/shard_map/qkv/pallas_call | solution.py:58
  232.6 75.9 %attn.3 = (bf16[1024,768]{1,0:T(8,128)(2,1)S(1)}, bf16[1024,768]{1,0:T(8,128)(2,1)S(1)}) custom-call(bf16[1024,768]{1,0:T(8,128)(2,1)S(1)} %get-tuple-element.29.refs_0_, bf16[1024,256]{1,0:T(8,128)(2,1)S(1)} %get-tuple-element.30.refs_1_), custom_call_target="tpu_custom_call" | custom-call | flops 12884901888 | bytes 4718592 | tf_op jit(solution)/shard_map/attn/pallas_call | solution.py:257
  308.6 2.3 copy-done.24
  311.0 7.1 %outproj.3 = (bf16[1024,1536]{1,0:T(8,128)(2,1)S(1)}, bf16[1024,1536]{1,0:T(8,128)(2,1)S(1)}) custom-call(s32[1]{0:T(128)} %bitcast.place_ref, bf16[1024,768]{1,0:T(8,128)(2,1)S(1)} %get-tuple-element.31.o_own_ref, bf16[1024,768]{1,0:T(8,128)(2,1)S(1)} %get-tuple-element.32.o_peer_ref, bf16[1024,1536]{1,0:T(8,128)(2,1)S(1)} %copy-done.22, ...), custom_call_target="tpu_custom_call" | custom-call | flops 4831838208 | bytes 20447232 | tf_op jit(solution)/shard_map/outproj/pallas_call | solution.py:302
  318.1 1.6 copy-done.25
  319.7 1.7 copy-done.26
  321.4 85.9 %mlp.3 = bf16[1024,1536]{1,0:T(8,128)(2,1)} custom-call(bf16[1024,1536]{1,0:T(8,128)(2,1)} %copy-done.26, bf16[1024,1536]{1,0:T(8,128)(2,1)} %copy-done.25, bf16[2,1536,4480]{2,1,0:T(8,128)(2,1)} %wg_hbm.3, bf16[2,1536,4480]{2,1,0:T(8,128)(2,1)} %wu_hbm.3, bf16[2,4480,1536]{2,1,0:T(8,128)(2,1)} %wd_hbm.3), custom_call_target="tpu_custom_call" | custom-call | flops 42278584320 | bytes 41287680 | tf_op jit(solution)/shard_map/mlp/pallas_call | solution.py:390
  407.3 3.8 copy.30
  (62 shorter events, 7.7 us)
Async XLA Ops:
  0.6 7.0 %copy-start.12 = (bf16[1024,1536]{1,0:T(8,128)(2,1)S(1)}, bf16[1024,1536]{1,0:T(8,128)(2,1)}, u32[]{:S(2)}) copy-start(bf16[1024,1536]{1,0:T(8,128)(2,1)} %x_ref.3) | copy-start | bytes 9437188
  0.6 6.9 %copy-start.13 = (bf16[2,1536,128]{2,1,0:T(8,128)(2,1)S(1)}, bf16[2,1536,128]{2,1,0:T(8,128)(2,1)}, u32[]{:S(2)}) copy-start(bf16[2,1536,128]{2,1,0:T(8,128)(2,1)} %wk_ref.3) | copy-start | bytes 2359300
  1.5 16.8 %copy-start.17 = (bf16[2,1,128]{2,1,0:T(2,128)(2,1)}, bf16[2,1,128]{2,1,0:T(2,128)(2,1)S(1)}, u32[]{:S(2)}) copy-start(bf16[2,1,128]{2,1,0:T(2,128)(2,1)S(1)} %copy.21.bk_ref) | copy-start | bytes 1540
  2.5 15.8 %copy-start.19 = (bf16[2,1,128]{2,1,0:T(2,128)(2,1)}, bf16[2,1,128]{2,1,0:T(2,128)(2,1)S(1)}, u32[]{:S(2)}) copy-start(bf16[2,1,128]{2,1,0:T(2,128)(2,1)S(1)} %copy.22.bv_ref) | copy-start | bytes 1540
  3.9 14.4 %copy-start.8 = (bf16[2,1,768]{2,1,0:T(2,128)(2,1)}, bf16[2,1,768]{2,1,0:T(2,128)(2,1)S(1)}, u32[]{:S(2)}) copy-start(bf16[2,1,768]{2,1,0:T(2,128)(2,1)S(1)} %copy.20.bq_ref) | copy-start | bytes 9220
  4.6 13.7 %copy-start.6 = (bf16[2,1,1536]{2,1,0:T(2,128)(2,1)}, bf16[2,1,1536]{2,1,0:T(2,128)(2,1)S(1)}, u32[]{:S(2)}) copy-start(bf16[2,1,1536]{2,1,0:T(2,128)(2,1)S(1)} %copy.19.gain_ref) | copy-start | bytes 18436
  5.3 107.5 %copy-start.4 = (bf16[2,1,1536]{2,1,0:T(2,128)(2,1)}, bf16[2,1,1536]{2,1,0:T(2,128)(2,1)S(1)}, u32[]{:S(2)}) copy-start(bf16[2,1,1536]{2,1,0:T(2,128)(2,1)S(1)} %copy.23.gain_ref) | copy-start | bytes 18436
  7.6 10.7 %copy-start = (f32[1024,128]{1,0:T(8,128)}, f32[1024,128]{1,0:T(8,128)S(1)}, u32[]{:S(2)}) copy-start(f32[1024,128]{1,0:T(8,128)S(1)} %get-tuple-element.42.cos_ref) | copy-start | bytes 1572868
  7.6 10.7 %copy-start.2 = (f32[1024,128]{1,0:T(8,128)}, f32[1024,128]{1,0:T(8,128)S(1)}, u32[]{:S(2)}) copy-start(f32[1024,128]{1,0:T(8,128)S(1)} %get-tuple-element.43.sin_ref) | copy-start | bytes 1572868
  7.6 2.7 copy-start.10
  11.4 101.4 %slice-start = ((s8[4718592]{0:T(1024)(128)(4,1)}), s8[4194304]{0:T(1024)(128)(4,1)S(1)}, s32[]{:S(2)}) async-start(s8[4718592]{0:T(1024)(128)(4,1)} %bitcast.10), calls=%async_computation | async-start | bytes 8388608
  18.3 94.5 %slice-start.1 = ((s8[4718592]{0:T(1024)(128)(4,1)}), s8[524288]{0:T(1024)(128)(4,1)S(1)}, s32[]{:S(2)}) async-start(s8[4718592]{0:T(1024)(128)(4,1)} %bitcast.10), calls=%async_computation.1 | async-start | bytes 1048576
  112.9 2.3 copy-start.23
  122.5 1.7 copy-start.27
  124.2 1.7 copy-start.28
  218.7 2.3 copy-start.11
  224.6 1.9 copy-start.21
  226.5 82.1 %slice-start.2 = ((s8[4718592]{0:T(1024)(128)(4,1)}), s8[4194304]{0:T(1024)(128)(4,1)S(1)}, s32[]{:S(2)}) async-start(s8[4718592]{0:T(1024)(128)(4,1)} %bitcast.12), calls=%async_computation.2 | async-start | bytes 8388608
  232.6 76.0 %copy-start.5 = (bf16[2,1,1536]{2,1,0:T(2,128)(2,1)S(1)}, bf16[2,1,1536]{2,1,0:T(2,128)(2,1)}, u32[]{:S(2)}) copy-start(bf16[2,1,1536]{2,1,0:T(2,128)(2,1)} %copy-done.4) | copy-start | bytes 18436
  232.6 76.0 %slice-start.3 = ((s8[4718592]{0:T(1024)(128)(4,1)}), s8[524288]{0:T(1024)(128)(4,1)S(1)}, s32[]{:S(2)}) async-start(s8[4718592]{0:T(1024)(128)(4,1)} %bitcast.12), calls=%async_computation.3 | async-start | bytes 1048576
  232.6 76.0 %copy-start.22 = (bf16[1024,1536]{1,0:T(8,128)(2,1)S(1)}, bf16[1024,1536]{1,0:T(8,128)(2,1)}, u32[]{:S(2)}) copy-start(bf16[1024,1536]{1,0:T(8,128)(2,1)} %mlp.2.x_ref) | copy-start | bytes 9437188
  308.6 2.3 copy-start.24
  318.1 1.6 copy-start.25
  319.7 1.7 copy-start.26
  (9 other events, 8.1 us)
where the time goes:
time: 419 us; the launch traced here: 411 us
  Pallas kernels  373 us (89%)
  local copies, waits for them, and re-layouts  34.1 us (8%)
    pallas_call x2, Pallas kernels, mlp(): pl.pallas_call(functools.partial(mlp_kernel, layer=layer, tiles=tiles, ch...  175 us
    pallas_call x2, Pallas kernels, attention(): pl.pallas_call(functools.partial(attn_kernel, bq=bq, window_blocks=window...  170 us
    unnamed x67, local copies, waits for them, and re-layouts  30.2 us
    pallas_call x2, Pallas kernels, out_project(): pl.pallas_call(functools.partial(out_kernel, layer=layer), grid_spec=pltp...  14.4 us
    pallas_call x2, Pallas kernels, qkv(): pl.pallas_call(qkv_kernel, grid=(rows // block,), in_specs=[out(width)] +...  13 us

commit v1 on v0

--- a/solution.py
+++ b/solution.py
@@ -67,13 +67,8 @@
     )(x, gain, wq, wk, wv, bq, bk, bv, cos_tab, sin_tab)
 
 
-def attn_kernel(*refs, bq, window_blocks, with_w):
-    refs = list(refs)
-    q_ref, kv_ref = refs[:2]; refs = refs[2:]
-    w_out = refs.pop(0) if with_w else None
-    o_ref, o_peer = refs[:2]; refs = refs[2:]
-    w_peer = refs.pop(0) if with_w else None
-    kv_buf, m_sc, l_sc, acc_sc, send_sems, recv_sems, o_send, o_recv, w_send, w_recv = refs
+def attn_kernel(*refs, layer, bq, window_blocks):
+    q_ref, kv_ref, w_out, o_ref, o_peer, w_peer, kv_buf, m_sc, l_sc, acc_sc, send_sems, recv_sems, o_send, o_recv, w_send, w_recv = refs
     rows = q_ref.shape[0]
     heads = q_ref.shape[1] // HEAD_DIM
     cp = lax.axis_index("cp")
@@ -100,11 +95,10 @@
         kv_copy(6, kv_buf.at[ynb, last], ynb, last, xnb),
         kv_copy(7, kv_buf.at[diag], diag, whole, mate),
     ]
-    if with_w:
-        quarter = w_out.shape[1] // 2
-        mine = pl.ds(pl.multiple_of(core * quarter, quarter), quarter)
-        w_z = pltpu.make_async_remote_copy(src_ref=w_out.at[:, mine], dst_ref=w_peer.at[:, mine], send_sem=w_send.at[0], recv_sem=w_recv.at[0], device_id={"tp": peer}, device_id_type=MESH)
-        w_d = pltpu.make_async_remote_copy(src_ref=w_peer.at[:, mine], dst_ref=w_peer.at[:, mine], send_sem=w_send.at[1], recv_sem=w_recv.at[1], device_id=at_cp(mate), device_id_type=MESH)
+    quarter = w_out.shape[1] // 2
+    mine = pl.ds(pl.multiple_of(core * quarter, quarter), quarter)
+    w_z = pltpu.make_async_remote_copy(src_ref=w_out.at[layer, mine], dst_ref=w_peer.at[mine], send_sem=w_send.at[0], recv_sem=w_recv.at[0], device_id={"tp": peer}, device_id_type=MESH)
+    w_d = pltpu.make_async_remote_copy(src_ref=w_peer.at[mine], dst_ref=w_peer.at[mine], send_sem=w_send.at[1], recv_sem=w_recv.at[1], device_id=at_cp(mate), device_id_type=MESH)
 
     barrier = pltpu.get_barrier_semaphore()
     for dev in (at_cp(mate), at_cp(xnb), at_cp(ynb), {"tp": peer}):
@@ -112,8 +106,7 @@
     pl.semaphore_wait(barrier, 4)
     for copy in kv_copies[:3]:
         copy.start()
-    if with_w:
-        w_z.start()
+    w_z.start()
 
     def o_copy(qb):
         part = pl.ds(pl.multiple_of(qb * bq, bq), bq)
@@ -226,101 +219,64 @@
         for h in range(heads):
             total = jnp.sum(l_sc[h], axis=1, keepdims=True)
             o_ref[pl.ds(q0, bq), h * HEAD_DIM:(h + 1) * HEAD_DIM] = (acc_sc[h] / total).astype(jnp.bfloat16)
-        o_copy(qb).start()
-        if with_w:
-            @pl.when(qb == 0)
-            def _():
-                w_z.wait_recv()
-                w_d.start()
+        @pl.when(qb < rows // bq - 1)
+        def _():
+            o_copy(qb).start()
+
+        @pl.when(qb == 0)
+        def _():
+            w_z.wait_recv()
+            w_d.start()
         return carry
 
     lax.fori_loop(0, rows // bq, q_block, 0)
     for copy in kv_copies:
         copy.wait_send()
-    if with_w:
-        w_z.wait_send()
-        w_d.wait()
-    for qb in range(rows // bq):
+    w_z.wait_send()
+    w_d.wait()
+    for qb in range(rows // bq - 1):
         o_copy(qb).wait()
 
-def attention(q, kv, w_out, window_blocks, bq, cid):
+def attention(layer, q, kv, w_out, window_blocks, bq, cid):
     rows, cols = q.shape
     heads = cols // HEAD_DIM
-    with_w = w_out is not None
     bf = jnp.bfloat16
     vm = pl.BlockSpec(memory_space=pltpu.VMEM)
     anys = pl.BlockSpec(memory_space=pl.ANY)
     nq = rows // bq
-    outs = [jax.ShapeDtypeStruct((rows, cols), bf), jax.ShapeDtypeStruct((rows, cols), bf)]
-    if with_w: outs.append(jax.ShapeDtypeStruct(w_out.shape, bf))
+    outs = [jax.ShapeDtypeStruct(sh, bf) for sh in ((rows, cols), (rows - bq, cols), w_out.shape[1:])]
     dma = pltpu.SemaphoreType.DMA
     return pl.pallas_call(
-        functools.partial(attn_kernel, bq=bq, window_blocks=window_blocks, with_w=with_w),
-        in_specs=[vm, vm] + [anys] * with_w,
-        out_specs=[vm, anys] + [anys] * with_w,
+        functools.partial(attn_kernel, layer=layer, bq=bq, window_blocks=window_blocks),
+        in_specs=[vm, vm, anys],
+        out_specs=[vm, anys, anys],
         out_shape=outs,
         scratch_shapes=[pltpu.VMEM((8, rows, 2 * HEAD_DIM), bf)] + [pltpu.VMEM((heads, bq, HEAD_DIM), jnp.float32)] * 3
         + [dma((8,)), dma((8,)), dma((nq,)), dma((nq,)), dma((2,)), dma((2,))],
         compiler_params=pltpu.CompilerParams(vmem_limit_bytes=48 * MIB, collective_id=cid, has_side_effects=True),
         cost_estimate=pl.CostEstimate(flops=16 * rows * rows * cols, bytes_accessed=rows * cols * 6, transcendentals=0),
         name="attn",
-    )(q, kv, *([w_out] if with_w else []))
-
-
-def out_kernel(place_ref, o_own_ref, o_peer_ref, x_ref, gain_ref, w_own_hbm, w_peer_hbm, x1_ref, h2_ref, w_full, o_full, sems, *, layer):
-    half = o_own_ref.shape[1]
-    own0 = pl.multiple_of(place_ref[0] * half, half)
-    peer0 = pl.multiple_of((1 - place_ref[0]) * half, half)
-
-    @pl.when(pl.program_id(0) == 0)
-    def _():
-        copies = [
-            pltpu.make_async_copy(w_own_hbm.at[layer], w_full.at[pl.ds(own0, half)], sems.at[0]),
-            pltpu.make_async_copy(w_peer_hbm.at[layer], w_full.at[pl.ds(peer0, half)], sems.at[1]),
-        ]
-        for copy in copies:
-            copy.start()
-        for copy in copies:
-            copy.wait()
-
-    o_full[:, pl.ds(own0, half)] = o_own_ref[...]
-    o_full[:, pl.ds(peer0, half)] = o_peer_ref[...]
-    prod = jnp.dot(o_full[...], w_full[...], preferred_element_type=jnp.float32)
-    x1 = (x_ref[...].astype(jnp.float32) + prod).astype(jnp.bfloat16)
-    x1_ref[...] = x1
-    h2_ref[...] = rms_rows(x1.astype(jnp.float32), gain_ref[...].astype(jnp.float32))
-
-
-def out_project(layer, place, o_own, o_peer, x, gain, w_own, w_peer):
+    )(q, kv, w_out)
+
+
+def tail_kernel(*refs, layer, tiles, chunks, head_rows, with_qkv):
+    refs = list(refs)
+    o_own, o_head, x_hbm, gain_ref, w_out, w_peer, wg_hbm, wu_hbm, wd_hbm = refs[:9]
+    refs = refs[9:]
+    if with_qkv:
+        again_ref, wq_hbm, wk_hbm, wv_hbm, bq_ref, bk_ref, bv_ref, cos_hbm, sin_hbm = refs[:9]
+        refs = refs[9:]
+    out_hbm = refs.pop(0)
+    if with_qkv:
+        q_hbm, k_hbm, v_hbm, kv_hbm = refs[:4]
+        refs = refs[4:]
+    w_full, o_full, hs, recv, xbuf, acc, wg, wu, wd, w_sems, in_sems, x_sems, o_sems, send_sems, recv_sems, out_sems, qkv_sems = refs
     rows, half = o_own.shape
-    width = x.shape[1]
-    block = min(rows, 256)
-
-    def rowspec(cols):
-        return pl.BlockSpec((block, cols), lambda i, s: (i, 0))
-
-    return pl.pallas_call(
-        functools.partial(out_kernel, layer=layer),
-        grid_spec=pltpu.PrefetchScalarGridSpec(
-            num_scalar_prefetch=1,
-            grid=(rows // block,),
-            in_specs=[
-                rowspec(half), rowspec(half), rowspec(width),
-                pl.BlockSpec((None, 1, width), lambda i, s: (layer, 0, 0)),
-                pl.BlockSpec(memory_space=pl.ANY), pl.BlockSpec(memory_space=pl.ANY),
-            ],
-            out_specs=[rowspec(width), rowspec(width)],
-            scratch_shapes=[pltpu.VMEM((2 * half, width), jnp.bfloat16), pltpu.VMEM((block, 2 * half), jnp.bfloat16), pltpu.SemaphoreType.DMA((2,))],
-        ),
-        out_shape=[jax.ShapeDtypeStruct((rows, width), jnp.bfloat16)] * 2,
-        compiler_params=pltpu.CompilerParams(vmem_limit_bytes=32 * MIB),
-        cost_estimate=pl.CostEstimate(flops=4 * rows * half * width, bytes_accessed=rows * width * 10 + 4 * half * width, transcendentals=0),
-        name="outproj",
-    )(place, o_own, o_peer, x, gain, w_own, w_peer)
-
-
-def mlp_kernel(h_ref, x1_hbm, wg_hbm, wu_hbm, wd_hbm, out_hbm, wg, wu, wd, send, recv, x1_buf, acc, w_sems, send_sems, recv_sems, x_sem, out_sems, *, layer, tiles, chunks):
-    peer = 1 - lax.axis_index("tp")
+    tp = lax.axis_index("tp")
+    peer = {"tp": 1 - tp}
+    own_cols = pl.ds(pl.multiple_of(tp * half, half), half)
+    peer_cols = pl.ds(pl.multiple_of((1 - tp) * half, half), half)
+    head_part, tail_part = pl.ds(0, head_rows), pl.ds(head_rows, rows - head_rows)
     offs = [sum(tiles[:i]) for i in range(len(tiles))]
     starts = [sum(chunks[:i]) for i in range(len(chunks))]
 
@@ -332,24 +288,51 @@
             pltpu.make_async_copy(wd_hbm.at[layer, c], wd.at[c], w_sems.at[i, 2]),
         )
 
+    def x_copy(ci):
+        n = chunks[ci]
+        return pltpu.make_async_copy(x_hbm.at[pl.ds(starts[ci], n)], xbuf.at[ci % 2, pl.ds(0, n)], x_sems.at[ci])
+
+    first = [
+        pltpu.make_async_copy(w_out.at[layer], w_full.at[own_cols], in_sems.at[0]),
+        pltpu.make_async_copy(w_peer, w_full.at[peer_cols], in_sems.at[1]),
+        pltpu.make_async_copy(o_own, o_full.at[:, own_cols], in_sems.at[2]),
+        pltpu.make_async_copy(o_head, o_full.at[head_part, peer_cols], in_sems.at[3]),
+        x_copy(0),
+    ]
+    for copy in first:
+        copy.start()
+    barrier = pltpu.get_barrier_semaphore()
+    pl.semaphore_signal(barrier, inc=1, device_id=peer, device_id_type=MESH)
+    pl.semaphore_wait(barrier, 1)
+    o_swap = pltpu.make_async_remote_copy(src_ref=o_own.at[tail_part], dst_ref=o_full.at[tail_part, own_cols], send_sem=o_sems.at[0], recv_sem=o_sems.at[1], device_id=peer, device_id_type=MESH)
+    o_swap.start()
     for i in range(len(tiles)):
         for copy in w_copies(i):
             copy.start()
-    x_copy = pltpu.make_async_copy(x1_hbm, x1_buf, x_sem.at[0])
-    x_copy.start()
-    barrier = pltpu.get_barrier_semaphore()
-    pl.semaphore_signal(barrier, inc=1, device_id={"tp": peer}, device_id_type=MESH)
-    pl.semaphore_wait(barrier, 1)
+    for copy in first:
+        copy.wait()
 
     swaps = []
+    tail_here = False
     for ci, n in enumerate(chunks):
         r = pl.ds(starts[ci], n)
+        if starts[ci] + n > head_rows and not tail_here:
+            o_swap.wait()
+            tail_here = True
+        if ci > 0:
+            x_copy(ci).wait()
+        if ci + 1 < len(chunks):
+            x_copy(ci + 1).start()
+        prod = jnp.dot(o_full[r, :], w_full[...], preferred_element_type=jnp.float32)
+        x1 = (xbuf[ci % 2, pl.ds(0, n), :].astype(jnp.float32) + prod).astype(jnp.bfloat16)
+        o_full[r, :] = x1
+        hs[r, :] = rms_rows(x1.astype(jnp.float32), gain_ref[...].astype(jnp.float32))
         for i, t in enumerate(tiles):
             if ci == 0:
                 for copy in w_copies(i):
                     copy.wait()
             c = pl.ds(offs[i], t)
-            normed = h_ref[r, :]
+            normed = hs[r, :]
             gate = jnp.dot(normed, wg[:, c], preferred_element_type=jnp.float32)
             up = jnp.dot(normed, wu[:, c], preferred_element_type=jnp.float32)
             act = (gate * jax.nn.sigmoid(gate) * up).astype(jnp.bfloat16)
@@ -359,49 +342,103 @@
             elif i < len(tiles) - 1:
                 acc[:n, :] += part
             else:
-                send[r, :] = (acc[:n, :] + part).astype(jnp.bfloat16)
-        swap = pltpu.make_async_remote_copy(src_ref=send.at[r], dst_ref=recv.at[r], send_sem=send_sems.at[ci], recv_sem=recv_sems.at[ci], device_id={"tp": peer}, device_id_type=MESH)
+                hs[r, :] = (acc[:n, :] + part).astype(jnp.bfloat16)
+        swap = pltpu.make_async_remote_copy(src_ref=hs.at[r], dst_ref=recv.at[r], send_sem=send_sems.at[ci], recv_sem=recv_sems.at[ci], device_id=peer, device_id_type=MESH)
         swap.start()
         swaps.append(swap)
 
-    x_copy.wait()
-    out_copies = []
+    waits = []
+    if with_qkv:
+        q_cols = wq_hbm.shape[2]
+        kv_cols = q_cols + 2 * HEAD_DIM
+        nxt = layer + 1
+        loads = [
+            pltpu.make_async_copy(wq_hbm.at[nxt], w_full.at[:, pl.ds(0, q_cols)], qkv_sems.at[0]),
+            pltpu.make_async_copy(wk_hbm.at[nxt], w_full.at[:, pl.ds(q_cols, HEAD_DIM)], qkv_sems.at[1]),
+            pltpu.make_async_copy(wv_hbm.at[nxt], w_full.at[:, pl.ds(q_cols + HEAD_DIM, HEAD_DIM)], qkv_sems.at[2]),
+        ]
+        for ci, n in enumerate(chunks):
+            r = pl.ds(starts[ci], n)
+            at = ci * 2 * HEAD_DIM
+            loads.append(pltpu.make_async_copy(cos_hbm.at[r], acc.at[pl.ds(0, n), pl.ds(at, HEAD_DIM)], qkv_sems.at[3 + 2 * ci]))
+            loads.append(pltpu.make_async_copy(sin_hbm.at[r], acc.at[pl.ds(0, n), pl.ds(at + HEAD_DIM, HEAD_DIM)], qkv_sems.at[4 + 2 * ci]))
+        for copy in loads:
+            copy.start()
+        for copy in loads:
+            copy.wait()
     for ci, n in enumerate(chunks):
         r = pl.ds(starts[ci], n)
         swaps[ci].wait()
-        total = send[r, :].astype(jnp.float32) + recv[r, :].astype(jnp.float32)
-        x1_buf[r, :] = (x1_buf[r, :].astype(jnp.float32) + total).astype(jnp.bfloat16)
-        out_copy = pltpu.make_async_copy(x1_buf.at[r], out_hbm.at[r], out_sems.at[ci])
-        out_copy.start()
-        out_copies.append(out_copy)
-    for out_copy in out_copies:
-        out_copy.wait()
-
-
-def mlp(layer, h2, x1, wg, wu, wd, cid):
-    rows, width = h2.shape
+        total = hs[r, :].astype(jnp.float32) + recv[r, :].astype(jnp.float32)
+        x2 = (o_full[r, :].astype(jnp.float32) + total).astype(jnp.bfloat16)
+        o_full[r, :] = x2
+        done = [pltpu.make_async_copy(o_full.at[r], out_hbm.at[r], out_sems.at[ci, 0])]
+        if with_qkv:
+            at = ci * 2 * HEAD_DIM
+            cos_tab = acc[:n, at:at + HEAD_DIM]
+            sin_tab = acc[:n, at + HEAD_DIM:at + 2 * HEAD_DIM]
+            normed = rms_rows(x2.astype(jnp.float32), again_ref[...].astype(jnp.float32))
+            proj = jnp.dot(normed, w_full[:, :kv_cols], preferred_element_type=jnp.float32)
+
+            def rope(cols, bias):
+                block = proj[:, cols] + bias
+                return (block * cos_tab + pltpu.roll(block, HEAD_DIM // 2, 1) * sin_tab).astype(jnp.bfloat16)
+
+            for at in range(0, q_cols, HEAD_DIM):
+                cols = slice(at, at + HEAD_DIM)
+                hs[r, cols] = rope(cols, bq_ref[:, cols].astype(jnp.float32))
+            k_cols, v_cols = slice(q_cols, q_cols + HEAD_DIM), slice(q_cols + HEAD_DIM, kv_cols)
+            hs[r, k_cols] = rope(k_cols, bk_ref[...].astype(jnp.float32))
+            hs[r, v_cols] = (proj[:, v_cols] + bv_ref[...].astype(jnp.float32)).astype(jnp.bfloat16)
+            done.append(pltpu.make_async_copy(hs.at[r, pl.ds(0, q_cols)], q_hbm.at[r], out_sems.at[ci, 1]))
+            done.append(pltpu.make_async_copy(hs.at[r, pl.ds(q_cols, HEAD_DIM)], k_hbm.at[r], out_sems.at[ci, 2]))
+            done.append(pltpu.make_async_copy(hs.at[r, pl.ds(q_cols + HEAD_DIM, HEAD_DIM)], v_hbm.at[r], out_sems.at[ci, 3]))
+            done.append(pltpu.make_async_copy(hs.at[r, pl.ds(q_cols, 2 * HEAD_DIM)], kv_hbm.at[r], out_sems.at[ci, 4]))
+        for copy in done:
+            copy.start()
+        waits += done
+    for copy in waits:
+        copy.wait()
+
+
+def layer_tail(layer, o_own, o_head, x, gain, w_out, w_peer, wg, wu, wd, next_qkv, cid):
+    rows, half = o_own.shape
+    width = x.shape[1]
     cols = wg.shape[2]
-    tiles = (256, 512, 768, 1024, 1024, 896)
+    tiles = (256, 512, 768, 768, 768, 768, 640)
     chunks = (256,) * (rows // 256)
     nt, nc = len(tiles), len(chunks)
     anys = pl.BlockSpec(memory_space=pl.ANY)
     bf = jnp.bfloat16
     dma = pltpu.SemaphoreType.DMA
+
+    def layer_row(a, l):
+        return pl.BlockSpec((None,) + a.shape[1:], lambda i: (l, 0, 0))
+
+    args = [o_own, o_head, x, gain, w_out, w_peer, wg, wu, wd]
+    specs = [anys] * 3 + [layer_row(gain, layer)] + [anys] * 5
+    outs = [jax.ShapeDtypeStruct((rows, width), bf)]
+    if next_qkv is not None:
+        again, wq, wk, wv, bq, bk, bv, cos_tab, sin_tab = next_qkv
+        args += list(next_qkv)
+        specs += [layer_row(again, layer + 1)] + [anys] * 3 + [layer_row(b, layer + 1) for b in (bq, bk, bv)] + [anys] * 2
+        outs += [jax.ShapeDtypeStruct((rows, c), bf) for c in (wq.shape[2], HEAD_DIM, HEAD_DIM, 2 * HEAD_DIM)]
     return pl.pallas_call(
-        functools.partial(mlp_kernel, layer=layer, tiles=tiles, chunks=chunks),
-        in_specs=[pl.BlockSpec(memory_space=pltpu.VMEM), anys, anys, anys, anys],
-        out_specs=anys,
-        out_shape=jax.ShapeDtypeStruct((rows, width), bf),
+        functools.partial(tail_kernel, layer=layer, tiles=tiles, chunks=chunks, head_rows=o_head.shape[0], with_qkv=next_qkv is not None),
+        grid=(1,),
+        in_specs=specs,
+        out_specs=[anys] * len(outs),
+        out_shape=outs,
         scratch_shapes=[
+            pltpu.VMEM((2 * half, width), bf), pltpu.VMEM((rows, width), bf), pltpu.VMEM((rows, width), bf), pltpu.VMEM((rows, width), bf),
+            pltpu.VMEM((2, max(chunks), width), bf), pltpu.VMEM((max(chunks), width), jnp.float32),
             pltpu.VMEM((width, cols), bf), pltpu.VMEM((width, cols), bf), pltpu.VMEM((cols, width), bf),
-            pltpu.VMEM((rows, width), bf), pltpu.VMEM((rows, width), bf), pltpu.VMEM((rows, width), bf),
-            pltpu.VMEM((max(chunks), width), jnp.float32),
-            dma((nt, 3)), dma((nc,)), dma((nc,)), dma((1,)), dma((nc,)),
+            dma((nt, 3)), dma((4,)), dma((nc,)), dma((2,)), dma((nc,)), dma((nc,)), dma((nc, 5)), dma((3 + 2 * nc,)),
         ],
         compiler_params=pltpu.CompilerParams(vmem_limit_bytes=67043328, collective_id=cid, has_side_effects=True),
         cost_estimate=pl.CostEstimate(flops=6 * rows * width * cols, bytes_accessed=6 * width * cols, transcendentals=0),
-        name="mlp",
-    )(h2, x1, wg, wu, wd)
+        name="tail",
+    )(*args)
 
 
 def solution(mesh):
@@ -409,7 +446,6 @@
 
     def local_step(x_in, positions, attn_gain, mlp_gain, w_query, b_query, w_key, b_key, w_value, b_value, w_out, w_gate, w_up, w_down):
         block_dev = x_in.shape[0]
-        tp = lax.axis_index("tp")
         inv_freq = 1.0 / (1000000.0 ** (jnp.arange(0, HEAD_DIM, 2, dtype=jnp.float32) / HEAD_DIM))
         angles = positions.astype(jnp.float32)[:, None] * inv_freq[None, :]
         cos_half, sin_half = jnp.cos(angles), jnp.sin(angles)
@@ -418,17 +454,16 @@
         row = lambda a: a[:, None, :]
         attn_gain, mlp_gain, b_query, b_key, b_value = (row(a) for a in (attn_gain, mlp_gain, b_query, b_key, b_value))
 
-        place = jnp.reshape(tp, (1,)).astype(jnp.int32)
-        hidden, w_peer, caches = x_in, None, []
+        qkv_args = (attn_gain, w_query, w_key, w_value, b_query, b_key, b_value, cos_tab, sin_tab)
+        hidden, caches = x_in, []
+        q, k, v, kv = qkv(0, hidden, *qkv_args)
         for layer, window_blocks in ((0, cp_size), (1, WINDOW // block_dev)):
-            q, k, v, kv = qkv(layer, hidden, attn_gain, w_query, w_key, w_value, b_query, b_key, b_value, cos_tab, sin_tab)
-            o, o_peer, *rest = attention(q, kv, w_out if layer == 0 else None, window_blocks, 512, 2 * layer)
-            if layer == 0:
-                w_peer = rest[0]
-            x1, h2 = out_project(layer, place, o, o_peer, hidden, mlp_gain, w_out, w_peer)
-            hidden = mlp(layer, h2, x1, w_gate, w_up, w_down, 2 * layer + 1)
             caches.append(k[:, None, :])
             caches.append(v[:, None, :])
+            o, o_head, w_peer = attention(layer, q, kv, w_out, window_blocks, 512, 2 * layer)
+            hidden, *rest = layer_tail(layer, o, o_head, hidden, mlp_gain, w_out, w_peer, w_gate, w_up, w_down, qkv_args if layer == 0 else None, 2 * layer + 1)
+            if layer == 0:
+                q, k, v, kv = rest
         return hidden, caches[0], caches[1], caches[2], caches[3]
 
     weight_col = P(None, None, "tp")

time: 419 us -> 334 us (0.80); the launches traced: 411 us -> 331 us
  Pallas kernels: 373 us -> 306 us
  local copies, waits for them, and re-layouts: 34.1 us -> 20.1 us
    pallas_call x6 -> x4, Pallas kernels: 360 us -> 300 us  [the longest x2 176 us: layer_tail(): pl.pallas_call(functools.partial(tail_kernel, layer=layer, tiles=tiles, c...]
    unnamed x67 -> x39, local copies, waits for them, and re-layouts: 30.2 us -> 15.6 us
    pallas_call x2 -> x1, Pallas kernels: 13 us -> 6.41 us  [qkv(): pl.pallas_call(qkv_kernel, grid=(rows // block,), in_specs=[out(width)] +...]
where the time goes in v1:
time: 334 us; the launch traced here: 331 us
  Pallas kernels  306 us (92%)
  local copies, waits for them, and re-layouts  20.1 us (6%)
    pallas_call x2, Pallas kernels, layer_tail(): pl.pallas_call(functools.partial(tail_kernel, layer=layer, tiles=tiles, c...  176 us
    pallas_call x2, Pallas kernels, attention(): pl.pallas_call(functools.partial(attn_kernel, layer=layer, bq=bq, window_...  124 us
    unnamed x39, local copies, waits for them, and re-layouts  15.6 us

profile of v1, /device:TPU:4, one launch (start us, length us, event | category | flops | bytes accessed | tf_op | source)
XLA Modules:
  0.0 330.6 jit_solution(5258015299805009620)
XLA Ops:
  0.7 0.8 copy.21.bk_ref.refs_14_
  1.5 1.0 copy.22.bv_ref.refs_15_
  2.5 0.7 convert_element_type.3
  3.2 0.7 copy.20.bq_ref.refs_13_
  3.9 0.7 copy.19.gain_ref.refs_9_
  4.6 1.3 copy.23.refs_3_
  5.9 1.9 fusion
  7.8 0.3 pad_maximum_fusion
  8.2 2.7 copy-done.4
  10.9 1.1 copy-done.7
  12.0 6.4 %qkv.1 = (bf16[1024,768]{1,0:T(8,128)(2,1)S(1)}, bf16[1024,128]{1,0:T(8,128)(2,1)}, bf16[1024,128]{1,0:T(8,128)(2,1)}, bf16[1024,256]{1,0:T(8,128)(2,1)S(1)}) custom-call(bf16[1024,1536]{1,0:T(8,128)(2,1)S(1)} %copy-done.5, bf16[2,1,1536]{2,1,0:T(2,128)(2,1)S(1)} %copy.19.gain_ref.refs_9_, bf16[2,1536,768]{2,1,0:T(8,128)(2,1)S(1)} %copy-done.4, ...), custom_call_target="tpu_custom_call" | custom-call | flops 3221225472 | bytes 9437184 | tf_op jit(solution)/shard_map/qkv/pallas_call | solution.py:58
  18.5 53.5 %attn.2 = (bf16[1024,768]{1,0:T(8,128)(2,1)S(1)}, bf16[512,768]{1,0:T(8,128)(2,1)S(1)}, bf16[768,1536]{1,0:T(8,128)(2,1)}) custom-call(bf16[1024,768]{1,0:T(8,128)(2,1)S(1)} %get-tuple-element.20.refs_0_, bf16[1024,256]{1,0:T(8,128)(2,1)S(1)} %get-tuple-element.21.refs_1_, bf16[2,768,1536]{2,1,0:T(8,128)(2,1)} %refs_4_.3), custom_call_target="tpu_custom_call" | custom-call | flops 12884901888 | bytes 4718592 | tf_op jit(solution)/shard_map/attn/pallas_call | solution.py:249
  72.0 1.1 copy-done.11
  73.1 0.9 copy-done.13
  74.0 88.2 %tail.2 = (bf16[1024,1536]{1,0:T(8,128)(2,1)}, bf16[1024,768]{1,0:T(8,128)(2,1)}, bf16[1024,128]{1,0:T(8,128)(2,1)}, bf16[1024,128]{1,0:T(8,128)(2,1)}, bf16[1024,256]{1,0:T(8,128)(2,1)}) custom-call(bf16[1024,768]{1,0:T(8,128)(2,1)} %copy-done.11, bf16[512,768]{1,0:T(8,128)(2,1)} %copy-done.13, bf16[1024,1536]{1,0:T(8,128)(2,1)} %refs_2_.4, ...), custom_call_target="tpu_custom_call" | custom-call | flops 42278584320 | bytes 41287680 | tf_op jit(solution)/shard_map/tail/pallas_call | solution.py:426
  162.2 1.4 copy-done.10
  163.6 1.0 copy-done.15
  164.7 70.8 %attn.3 = (bf16[1024,768]{1,0:T(8,128)(2,1)S(1)}, bf16[512,768]{1,0:T(8,128)(2,1)S(1)}, bf16[768,1536]{1,0:T(8,128)(2,1)}) custom-call(bf16[1024,768]{1,0:T(8,128)(2,1)S(1)} %copy-done.10, bf16[1024,256]{1,0:T(8,128)(2,1)S(1)} %copy-done.15, bf16[2,768,1536]{2,1,0:T(8,128)(2,1)} %refs_4_.3), custom_call_target="tpu_custom_call" | custom-call | flops 12884901888 | bytes 4718592 | tf_op jit(solution)/shard_map/attn/pallas_call | solution.py:249
  235.5 1.1 copy-done.12
  236.6 0.9 copy-done.14
  237.6 87.4 %tail.3 = bf16[1024,1536]{1,0:T(8,128)(2,1)} custom-call(bf16[1024,768]{1,0:T(8,128)(2,1)} %copy-done.12, bf16[512,768]{1,0:T(8,128)(2,1)} %copy-done.14, bf16[1024,1536]{1,0:T(8,128)(2,1)} %get-tuple-element.29.refs_2_, bf16[2,1,1536]{2,1,0:T(2,128)(2,1)} %copy.23.refs_3_, bf16[2,768,1536]{2,1,0:T(8,128)(2,1)} %refs_4_.3, ...), custom_call_target="tpu_custom_call" | custom-call | flops 42278584320 | bytes 41287680 | tf_op jit(solution)/shard_map/tail/pallas_call | solution.py:426
  325.0 3.8 %copy.32 = bf16[1024,1536]{1,0:T(8,128)(2,1)} copy(bf16[1024,1536]{1,0:T(8,128)(2,1)} %tail.3) | data formatting | bytes 6291456
  328.8 0.7 copy.33
  329.5 0.7 copy.34
  (29 shorter events, 0.1 us)
Async XLA Ops:
  0.6 7.5 %copy-start.6 = (bf16[2,1536,128]{2,1,0:T(8,128)(2,1)S(1)}, bf16[2,1536,128]{2,1,0:T(8,128)(2,1)}, u32[]{:S(2)}) copy-start(bf16[2,1536,128]{2,1,0:T(8,128)(2,1)} %refs_11_.1) | copy-start | bytes 2359300
  0.6 7.5 %copy-start.5 = (bf16[1024,1536]{1,0:T(8,128)(2,1)S(1)}, bf16[1024,1536]{1,0:T(8,128)(2,1)}, u32[]{:S(2)}) copy-start(bf16[1024,1536]{1,0:T(8,128)(2,1)} %refs_2_.4) | copy-start | bytes 9437188
  1.5 17.0 %copy-start.8 = (bf16[2,1,128]{2,1,0:T(2,128)(2,1)}, bf16[2,1,128]{2,1,0:T(2,128)(2,1)S(1)}, u32[]{:S(2)}) copy-start(bf16[2,1,128]{2,1,0:T(2,128)(2,1)S(1)} %copy.21.bk_ref.refs_14_) | copy-start | bytes 1540
  2.5 15.9 %copy-start.9 = (bf16[2,1,128]{2,1,0:T(2,128)(2,1)}, bf16[2,1,128]{2,1,0:T(2,128)(2,1)S(1)}, u32[]{:S(2)}) copy-start(bf16[2,1,128]{2,1,0:T(2,128)(2,1)S(1)} %copy.22.bv_ref.refs_15_) | copy-start | bytes 1540
  3.9 14.6 %copy-start.3 = (bf16[2,1,768]{2,1,0:T(2,128)(2,1)}, bf16[2,1,768]{2,1,0:T(2,128)(2,1)S(1)}, u32[]{:S(2)}) copy-start(bf16[2,1,768]{2,1,0:T(2,128)(2,1)S(1)} %copy.20.bq_ref.refs_13_) | copy-start | bytes 9220
  4.6 13.9 %copy-start.2 = (bf16[2,1,1536]{2,1,0:T(2,128)(2,1)}, bf16[2,1,1536]{2,1,0:T(2,128)(2,1)S(1)}, u32[]{:S(2)}) copy-start(bf16[2,1,1536]{2,1,0:T(2,128)(2,1)S(1)} %copy.19.gain_ref.refs_9_) | copy-start | bytes 18436
  8.1 10.3 %copy-start = (f32[1024,128]{1,0:T(8,128)}, f32[1024,128]{1,0:T(8,128)S(1)}, u32[]{:S(2)}) copy-start(f32[1024,128]{1,0:T(8,128)S(1)} %get-tuple-element.38.cos_ref.refs_16_) | copy-start | bytes 1572868
  8.2 10.3 %copy-start.1 = (f32[1024,128]{1,0:T(8,128)}, f32[1024,128]{1,0:T(8,128)S(1)}, u32[]{:S(2)}) copy-start(f32[1024,128]{1,0:T(8,128)S(1)} %get-tuple-element.39.sin_ref.refs_17_) | copy-start | bytes 1572868
  8.2 2.7 copy-start.4
  10.9 1.1 copy-start.7
  72.0 1.1 copy-start.11
  73.1 0.9 copy-start.13
  162.2 1.4 copy-start.10
  163.6 1.0 copy-start.15
  235.5 1.1 copy-start.12
  236.6 0.9 copy-start.14
  324.9 3.8 %copy-start.17 = (bf16[1024,128]{1,0:T(8,128)(2,1)S(1)}, bf16[1024,128]{1,0:T(8,128)(2,1)}, u32[]{:S(2)}) copy-start(bf16[1024,128]{1,0:T(8,128)(2,1)} %get-tuple-element.33) | copy-start | bytes 786436
  325.0 4.5 %copy-start.16 = (bf16[1024,128]{1,0:T(8,128)(2,1)S(1)}, bf16[1024,128]{1,0:T(8,128)(2,1)}, u32[]{:S(2)}) copy-start(bf16[1024,128]{1,0:T(8,128)(2,1)} %get-tuple-element.34) | copy-start | bytes 786436

commit v2 on v1

--- a/solution.py
+++ b/solution.py
@@ -19,56 +19,87 @@
     return (hidden_f * lax.rsqrt(variance + 1e-6) * gain_f).astype(jnp.bfloat16)
 
 
-def qkv_kernel(x_ref, gain_ref, wq_ref, wk_ref, wv_ref, bq_ref, bk_ref, bv_ref, cos_ref, sin_ref, q_ref, k_ref, v_ref, kv_ref):
-    normed = rms_rows(x_ref[...].astype(jnp.float32), gain_ref[...].astype(jnp.float32))
-    cos_tab = cos_ref[...]
-    sin_tab = sin_ref[...]
-
-    def rope(block):
-        return (block * cos_tab + pltpu.roll(block, HEAD_DIM // 2, 1) * sin_tab).astype(jnp.bfloat16)
-
-    k_f = jnp.dot(normed, wk_ref[...], preferred_element_type=jnp.float32) + bk_ref[...].astype(jnp.float32)
-    k_b = rope(k_f)
-    k_ref[...] = k_b
-    kv_ref[:, :HEAD_DIM] = k_b
-    v_f = jnp.dot(normed, wv_ref[...], preferred_element_type=jnp.float32) + bv_ref[...].astype(jnp.float32)
-    v_b = v_f.astype(jnp.bfloat16)
-    v_ref[...] = v_b
-    kv_ref[:, HEAD_DIM:] = v_b
-    q_f = jnp.dot(normed, wq_ref[...], preferred_element_type=jnp.float32) + bq_ref[...].astype(jnp.float32)
-    for head in range(q_ref.shape[1] // HEAD_DIM):
-        cols = slice(head * HEAD_DIM, (head + 1) * HEAD_DIM)
-        q_ref[:, cols] = rope(q_f[:, cols])
-
-
-def qkv(layer, x, gain, wq, wk, wv, bq, bk, bv, cos_tab, sin_tab):
+def qkv_kernel(x_hbm, gain_ref, wq_hbm, wk_hbm, wv_hbm, bq_ref, bk_ref, bv_ref, cos_ref, sin_ref, q_ref, k_hbm, v_hbm, kv_ref, x_buf, w_buf, w_sems, x_sems, kv_sems, *, chunks):
+    q_cols = wq_hbm.shape[2]
+    k_cols, v_cols = slice(q_cols, q_cols + HEAD_DIM), slice(q_cols + HEAD_DIM, q_cols + 2 * HEAD_DIM)
+    loads = [
+        pltpu.make_async_copy(wq_hbm.at[0], w_buf.at[:, pl.ds(0, q_cols)], w_sems.at[0]),
+        pltpu.make_async_copy(wk_hbm.at[0], w_buf.at[:, pl.ds(q_cols, HEAD_DIM)], w_sems.at[1]),
+        pltpu.make_async_copy(wv_hbm.at[0], w_buf.at[:, pl.ds(q_cols + HEAD_DIM, HEAD_DIM)], w_sems.at[2]),
+    ]
+    rows = x_hbm.shape[0] // chunks
+
+    def part(i):
+        return pl.ds(pl.multiple_of(i * rows, rows), rows)
+
+    def x_load(i):
+        return pltpu.make_async_copy(x_hbm.at[part(i)], x_buf.at[part(i)], x_sems.at[i])
+
+    x_load(0).start()
+    for copy in loads:
+        copy.start()
+    for i in range(1, chunks):
+        x_load(i).start()
+    gain = gain_ref[...].astype(jnp.float32)[:1]
+    b_q, b_k, b_v = (b[...].astype(jnp.float32)[:1] for b in (bq_ref, bk_ref, bv_ref))
+
+    def run_part(i, carry):
+        r = part(i)
+        x_load(i).wait()
+        normed = rms_rows(x_buf[r, :].astype(jnp.float32), gain)
+
+        @pl.when(i == 0)
+        def _():
+            for copy in loads:
+                copy.wait()
+
+        proj = jnp.dot(normed, w_buf[...], preferred_element_type=jnp.float32)
+        cos_tab, sin_tab = cos_ref[r, :], sin_ref[r, :]
+
+        def rope(cols, bias):
+            block = proj[:, cols] + bias
+            return (block * cos_tab + pltpu.roll(block, HEAD_DIM // 2, 1) * sin_tab).astype(jnp.bfloat16)
+
+        for at in range(0, q_cols, HEAD_DIM):
+            cols = slice(at, at + HEAD_DIM)
+            q_ref[r, cols] = rope(cols, b_q[:, cols])
+        kv_ref[r, :HEAD_DIM] = rope(k_cols, b_k)
+        kv_ref[r, HEAD_DIM:] = (proj[:, v_cols] + b_v).astype(jnp.bfloat16)
+        return carry
+
+    lax.fori_loop(0, chunks, run_part, 0)
+    stores = [
+        pltpu.make_async_copy(kv_ref.at[:, pl.ds(0, HEAD_DIM)], k_hbm, kv_sems.at[0]),
+        pltpu.make_async_copy(kv_ref.at[:, pl.ds(HEAD_DIM, HEAD_DIM)], v_hbm, kv_sems.at[1]),
+    ]
+    for copy in stores:
+        copy.start()
+    for copy in stores:
+        copy.wait()
+
+
+def qkv(x, gain, wq, wk, wv, bq, bk, bv, cos_tab, sin_tab):
     rows, width = x.shape
     q_cols = wq.shape[2]
-    block = min(rows, 256)
-
-    def whole(w):
-        return pl.BlockSpec((None,) + w.shape[1:], lambda i: (layer, 0, 0))
-
-    def table():
-        return pl.BlockSpec((block, HEAD_DIM), lambda i: (i, 0))
-
-    def out(cols):
-        return pl.BlockSpec((block, cols), lambda i: (i, 0))
-
+    chunks = 4
+    vm = pl.BlockSpec(memory_space=pltpu.VMEM)
+    hbm = pl.BlockSpec(memory_space=pltpu.HBM)
+    anys = pl.BlockSpec(memory_space=pl.ANY)
+    dma = pltpu.SemaphoreType.DMA
     return pl.pallas_call(
-        qkv_kernel,
-        grid=(rows // block,),
-        in_specs=[out(width)] + [whole(w) for w in (gain, wq, wk, wv, bq, bk, bv)] + [table(), table()],
-        out_specs=[out(c) for c in (q_cols, HEAD_DIM, HEAD_DIM, 2 * HEAD_DIM)],
+        functools.partial(qkv_kernel, chunks=chunks),
+        in_specs=[anys, vm, anys, anys, anys] + [vm] * 5,
+        out_specs=[vm, hbm, hbm, vm],
         out_shape=[jax.ShapeDtypeStruct((rows, c), jnp.bfloat16) for c in (q_cols, HEAD_DIM, HEAD_DIM, 2 * HEAD_DIM)],
-        compiler_params=pltpu.CompilerParams(vmem_limit_bytes=32 * MIB),
+        scratch_shapes=[pltpu.VMEM((rows, width), jnp.bfloat16), pltpu.VMEM((width, q_cols + 2 * HEAD_DIM), jnp.bfloat16), dma((3,)), dma((chunks,)), dma((2,))],
+        compiler_params=pltpu.CompilerParams(vmem_limit_bytes=48 * MIB),
         cost_estimate=pl.CostEstimate(flops=2 * rows * width * (q_cols + 256), bytes_accessed=rows * width * 4 + width * 2048, transcendentals=0),
         name="qkv",
     )(x, gain, wq, wk, wv, bq, bk, bv, cos_tab, sin_tab)
 
 
 def attn_kernel(*refs, layer, bq, window_blocks):
-    q_ref, kv_ref, w_out, o_ref, o_peer, w_peer, kv_buf, m_sc, l_sc, acc_sc, send_sems, recv_sems, o_send, o_recv, w_send, w_recv = refs
+    q_ref, kv_ref, w_out, o_hbm, o_peer, w_peer, kv_buf, o_ref, m_sc, l_sc, acc_sc, send_sems, recv_sems, o_send, o_recv, o_out, w_send, w_recv = refs
     rows = q_ref.shape[0]
     heads = q_ref.shape[1] // HEAD_DIM
     cp = lax.axis_index("cp")
@@ -112,6 +143,10 @@
         part = pl.ds(pl.multiple_of(qb * bq, bq), bq)
         return pltpu.make_async_remote_copy(src_ref=o_ref.at[part], dst_ref=o_peer.at[part], send_sem=o_send.at[qb], recv_sem=o_recv.at[qb], device_id={"tp": peer}, device_id_type=MESH)
 
+    def o_store(qb):
+        part = pl.ds(pl.multiple_of(qb * bq, bq), bq)
+        return pltpu.make_async_copy(o_ref.at[part], o_hbm.at[part], o_out.at[qb])
+
     def block(q0, kb, vb, keep):
         bk = kb.shape[0]
 
@@ -219,6 +254,8 @@
         for h in range(heads):
             total = jnp.sum(l_sc[h], axis=1, keepdims=True)
             o_ref[pl.ds(q0, bq), h * HEAD_DIM:(h + 1) * HEAD_DIM] = (acc_sc[h] / total).astype(jnp.bfloat16)
+        o_store(qb).start()
+
         @pl.when(qb < rows // bq - 1)
         def _():
             o_copy(qb).start()
@@ -234,6 +271,8 @@
         copy.wait_send()
     w_z.wait_send()
     w_d.wait()
+    for qb in range(rows // bq):
+        o_store(qb).wait()
     for qb in range(rows // bq - 1):
         o_copy(qb).wait()
 
@@ -249,17 +288,17 @@
     return pl.pallas_call(
         functools.partial(attn_kernel, layer=layer, bq=bq, window_blocks=window_blocks),
         in_specs=[vm, vm, anys],
-        out_specs=[vm, anys, anys],
+        out_specs=[pl.BlockSpec(memory_space=pltpu.HBM)] * 3,
         out_shape=outs,
-        scratch_shapes=[pltpu.VMEM((8, rows, 2 * HEAD_DIM), bf)] + [pltpu.VMEM((heads, bq, HEAD_DIM), jnp.float32)] * 3
-        + [dma((8,)), dma((8,)), dma((nq,)), dma((nq,)), dma((2,)), dma((2,))],
-        compiler_params=pltpu.CompilerParams(vmem_limit_bytes=48 * MIB, collective_id=cid, has_side_effects=True),
+        scratch_shapes=[pltpu.VMEM((8, rows, 2 * HEAD_DIM), bf), pltpu.VMEM((rows, cols), bf)] + [pltpu.VMEM((heads, bq, HEAD_DIM), jnp.float32)] * 3
+        + [dma((8,)), dma((8,)), dma((nq,)), dma((nq,)), dma((nq,)), dma((2,)), dma((2,))],
+        compiler_params=pltpu.CompilerParams(vmem_limit_bytes=67043328, collective_id=cid, has_side_effects=True),
         cost_estimate=pl.CostEstimate(flops=16 * rows * rows * cols, bytes_accessed=rows * cols * 6, transcendentals=0),
         name="attn",
     )(q, kv, w_out)
 
 
-def tail_kernel(*refs, layer, tiles, chunks, head_rows, with_qkv):
+def tail_kernel(*refs, layer, tile, chunk, head_rows, with_qkv):
     refs = list(refs)
     o_own, o_head, x_hbm, gain_ref, w_out, w_peer, wg_hbm, wu_hbm, wd_hbm = refs[:9]
     refs = refs[9:]
@@ -272,25 +311,29 @@
         refs = refs[4:]
     w_full, o_full, hs, recv, xbuf, acc, wg, wu, wd, w_sems, in_sems, x_sems, o_sems, send_sems, recv_sems, out_sems, qkv_sems = refs
     rows, half = o_own.shape
+    n_chunks, n_tiles = rows // chunk, wg_hbm.shape[2] // tile
     tp = lax.axis_index("tp")
     peer = {"tp": 1 - tp}
     own_cols = pl.ds(pl.multiple_of(tp * half, half), half)
     peer_cols = pl.ds(pl.multiple_of((1 - tp) * half, half), half)
     head_part, tail_part = pl.ds(0, head_rows), pl.ds(head_rows, rows - head_rows)
-    offs = [sum(tiles[:i]) for i in range(len(tiles))]
-    starts = [sum(chunks[:i]) for i in range(len(chunks))]
-
     def w_copies(i):
-        c = pl.ds(offs[i], tiles[i])
+        c = pl.ds(pl.multiple_of(i * tile, tile), tile)
         return (
             pltpu.make_async_copy(wg_hbm.at[layer, :, c], wg.at[:, c], w_sems.at[i, 0]),
             pltpu.make_async_copy(wu_hbm.at[layer, :, c], wu.at[:, c], w_sems.at[i, 1]),
             pltpu.make_async_copy(wd_hbm.at[layer, c], wd.at[c], w_sems.at[i, 2]),
         )
 
+    def chunk_rows(ci):
+        return pl.ds(pl.multiple_of(ci * chunk, chunk), chunk)
+
     def x_copy(ci):
-        n = chunks[ci]
-        return pltpu.make_async_copy(x_hbm.at[pl.ds(starts[ci], n)], xbuf.at[ci % 2, pl.ds(0, n)], x_sems.at[ci])
+        return pltpu.make_async_copy(x_hbm.at[chunk_rows(ci)], xbuf.at[lax.rem(ci, 2)], x_sems.at[ci])
+
+    def swap(ci):
+        r = chunk_rows(ci)
+        return pltpu.make_async_remote_copy(src_ref=hs.at[r], dst_ref=recv.at[r], send_sem=send_sems.at[ci], recv_sem=recv_sems.at[ci], device_id=peer, device_id_type=MESH)
 
     first = [
         pltpu.make_async_copy(w_out.at[layer], w_full.at[own_cols], in_sems.at[0]),
@@ -306,78 +349,94 @@
     pl.semaphore_wait(barrier, 1)
     o_swap = pltpu.make_async_remote_copy(src_ref=o_own.at[tail_part], dst_ref=o_full.at[tail_part, own_cols], send_sem=o_sems.at[0], recv_sem=o_sems.at[1], device_id=peer, device_id_type=MESH)
     o_swap.start()
-    for i in range(len(tiles)):
+    for i in range(n_tiles):
         for copy in w_copies(i):
             copy.start()
     for copy in first:
         copy.wait()
 
-    swaps = []
-    tail_here = False
-    for ci, n in enumerate(chunks):
-        r = pl.ds(starts[ci], n)
-        if starts[ci] + n > head_rows and not tail_here:
+    def run_chunk(ci, carry):
+        r = chunk_rows(ci)
+
+        @pl.when(ci == head_rows // chunk)
+        def _():
             o_swap.wait()
-            tail_here = True
-        if ci > 0:
+
+        @pl.when(ci > 0)
+        def _():
             x_copy(ci).wait()
-        if ci + 1 < len(chunks):
+
+        @pl.when(ci + 1 < n_chunks)
+        def _():
             x_copy(ci + 1).start()
+
         prod = jnp.dot(o_full[r, :], w_full[...], preferred_element_type=jnp.float32)
-        x1 = (xbuf[ci % 2, pl.ds(0, n), :].astype(jnp.float32) + prod).astype(jnp.bfloat16)
+        x1 = (xbuf[lax.rem(ci, 2)].astype(jnp.float32) + prod).astype(jnp.bfloat16)
         o_full[r, :] = x1
-        hs[r, :] = rms_rows(x1.astype(jnp.float32), gain_ref[...].astype(jnp.float32))
-        for i, t in enumerate(tiles):
-            if ci == 0:
+        hs[r, :] = rms_rows(x1.astype(jnp.float32), gain_ref[...].astype(jnp.float32)[layer:layer + 1])
+        acc[...] = jnp.zeros(acc.shape, jnp.float32)
+
+        def run_tile(i, c0):
+            @pl.when(ci == 0)
+            def _():
                 for copy in w_copies(i):
                     copy.wait()
-            c = pl.ds(offs[i], t)
+
+            c = pl.ds(pl.multiple_of(i * tile, tile), tile)
             normed = hs[r, :]
             gate = jnp.dot(normed, wg[:, c], preferred_element_type=jnp.float32)
             up = jnp.dot(normed, wu[:, c], preferred_element_type=jnp.float32)
             act = (gate * jax.nn.sigmoid(gate) * up).astype(jnp.bfloat16)
-            part = jnp.dot(act, wd[c, :], preferred_element_type=jnp.float32)
-            if i == 0:
-                acc[:n, :] = part
-            elif i < len(tiles) - 1:
-                acc[:n, :] += part
-            else:
-                hs[r, :] = (acc[:n, :] + part).astype(jnp.bfloat16)
-        swap = pltpu.make_async_remote_copy(src_ref=hs.at[r], dst_ref=recv.at[r], send_sem=send_sems.at[ci], recv_sem=recv_sems.at[ci], device_id=peer, device_id_type=MESH)
-        swap.start()
-        swaps.append(swap)
-
-    waits = []
+            acc[...] += jnp.dot(act, wd[c, :], preferred_element_type=jnp.float32)
+            return c0
+
+        lax.fori_loop(0, n_tiles, run_tile, 0)
+        hs[r, :] = acc[...].astype(jnp.bfloat16)
+        swap(ci).start()
+        return carry
+
+    lax.fori_loop(0, n_chunks, run_chunk, 0)
+
     if with_qkv:
         q_cols = wq_hbm.shape[2]
         kv_cols = q_cols + 2 * HEAD_DIM
         nxt = layer + 1
+        b_q, b_k, b_v = (b[...].astype(jnp.float32)[nxt:nxt + 1] for b in (bq_ref, bk_ref, bv_ref))
         loads = [
             pltpu.make_async_copy(wq_hbm.at[nxt], w_full.at[:, pl.ds(0, q_cols)], qkv_sems.at[0]),
             pltpu.make_async_copy(wk_hbm.at[nxt], w_full.at[:, pl.ds(q_cols, HEAD_DIM)], qkv_sems.at[1]),
             pltpu.make_async_copy(wv_hbm.at[nxt], w_full.at[:, pl.ds(q_cols + HEAD_DIM, HEAD_DIM)], qkv_sems.at[2]),
         ]
-        for ci, n in enumerate(chunks):
-            r = pl.ds(starts[ci], n)
+        for ci in range(n_chunks):
+            r = pl.ds(ci * chunk, chunk)
             at = ci * 2 * HEAD_DIM
-            loads.append(pltpu.make_async_copy(cos_hbm.at[r], acc.at[pl.ds(0, n), pl.ds(at, HEAD_DIM)], qkv_sems.at[3 + 2 * ci]))
-            loads.append(pltpu.make_async_copy(sin_hbm.at[r], acc.at[pl.ds(0, n), pl.ds(at + HEAD_DIM, HEAD_DIM)], qkv_sems.at[4 + 2 * ci]))
+            loads.append(pltpu.make_async_copy(cos_hbm.at[r], acc.at[:, pl.ds(at, HEAD_DIM)], qkv_sems.at[3 + 2 * ci]))
+            loads.append(pltpu.make_async_copy(sin_hbm.at[r], acc.at[:, pl.ds(at + HEAD_DIM, HEAD_DIM)], qkv_sems.at[4 + 2 * ci]))
         for copy in loads:
             copy.start()
         for copy in loads:
             copy.wait()
-    for ci, n in enumerate(chunks):
-        r = pl.ds(starts[ci], n)
-        swaps[ci].wait()
+    def out_copies(ci):
+        r = chunk_rows(ci)
+        copies = [pltpu.make_async_copy(o_full.at[r], out_hbm.at[r], out_sems.at[ci, 0])]
+        if with_qkv:
+            copies.append(pltpu.make_async_copy(hs.at[r, pl.ds(0, q_cols)], q_hbm.at[r], out_sems.at[ci, 1]))
+            copies.append(pltpu.make_async_copy(hs.at[r, pl.ds(q_cols, HEAD_DIM)], k_hbm.at[r], out_sems.at[ci, 2]))
+            copies.append(pltpu.make_async_copy(hs.at[r, pl.ds(q_cols + HEAD_DIM, HEAD_DIM)], v_hbm.at[r], out_sems.at[ci, 3]))
+            copies.append(pltpu.make_async_copy(hs.at[r, pl.ds(q_cols, 2 * HEAD_DIM)], kv_hbm.at[r], out_sems.at[ci, 4]))
+        return copies
+
+    def finish_chunk(ci, carry):
+        r = chunk_rows(ci)
+        swap(ci).wait()
         total = hs[r, :].astype(jnp.float32) + recv[r, :].astype(jnp.float32)
         x2 = (o_full[r, :].astype(jnp.float32) + total).astype(jnp.bfloat16)
         o_full[r, :] = x2
-        done = [pltpu.make_async_copy(o_full.at[r], out_hbm.at[r], out_sems.at[ci, 0])]
         if with_qkv:
             at = ci * 2 * HEAD_DIM
-            cos_tab = acc[:n, at:at + HEAD_DIM]
-            sin_tab = acc[:n, at + HEAD_DIM:at + 2 * HEAD_DIM]
-            normed = rms_rows(x2.astype(jnp.float32), again_ref[...].astype(jnp.float32))
+            cos_tab = acc[:, pl.ds(pl.multiple_of(at, HEAD_DIM), HEAD_DIM)]
+            sin_tab = acc[:, pl.ds(pl.multiple_of(at + HEAD_DIM, HEAD_DIM), HEAD_DIM)]
+            normed = rms_rows(x2.astype(jnp.float32), again_ref[...].astype(jnp.float32)[nxt:nxt + 1])
             proj = jnp.dot(normed, w_full[:, :kv_cols], preferred_element_type=jnp.float32)
 
             def rope(cols, bias):
@@ -386,52 +445,47 @@
 
             for at in range(0, q_cols, HEAD_DIM):
                 cols = slice(at, at + HEAD_DIM)
-                hs[r, cols] = rope(cols, bq_ref[:, cols].astype(jnp.float32))
+                hs[r, cols] = rope(cols, b_q[:, cols])
             k_cols, v_cols = slice(q_cols, q_cols + HEAD_DIM), slice(q_cols + HEAD_DIM, kv_cols)
-            hs[r, k_cols] = rope(k_cols, bk_ref[...].astype(jnp.float32))
-            hs[r, v_cols] = (proj[:, v_cols] + bv_ref[...].astype(jnp.float32)).astype(jnp.bfloat16)
-            done.append(pltpu.make_async_copy(hs.at[r, pl.ds(0, q_cols)], q_hbm.at[r], out_sems.at[ci, 1]))
-            done.append(pltpu.make_async_copy(hs.at[r, pl.ds(q_cols, HEAD_DIM)], k_hbm.at[r], out_sems.at[ci, 2]))
-            done.append(pltpu.make_async_copy(hs.at[r, pl.ds(q_cols + HEAD_DIM, HEAD_DIM)], v_hbm.at[r], out_sems.at[ci, 3]))
-            done.append(pltpu.make_async_copy(hs.at[r, pl.ds(q_cols, 2 * HEAD_DIM)], kv_hbm.at[r], out_sems.at[ci, 4]))
-        for copy in done:
+            hs[r, k_cols] = rope(k_cols, b_k)
+            hs[r, v_cols] = (proj[:, v_cols] + b_v).astype(jnp.bfloat16)
+        for copy in out_copies(ci):
             copy.start()
-        waits += done
-    for copy in waits:
-        copy.wait()
+        return carry
+
+    lax.fori_loop(0, n_chunks, finish_chunk, 0)
+    for ci in range(n_chunks):
+        for copy in out_copies(ci):
+            copy.wait()
 
 
 def layer_tail(layer, o_own, o_head, x, gain, w_out, w_peer, wg, wu, wd, next_qkv, cid):
     rows, half = o_own.shape
     width = x.shape[1]
     cols = wg.shape[2]
-    tiles = (256, 512, 768, 768, 768, 768, 640)
-    chunks = (256,) * (rows // 256)
-    nt, nc = len(tiles), len(chunks)
+    tile, chunk = 896, 256
+    nt, nc = cols // tile, rows // chunk
     anys = pl.BlockSpec(memory_space=pl.ANY)
     bf = jnp.bfloat16
     dma = pltpu.SemaphoreType.DMA
 
-    def layer_row(a, l):
-        return pl.BlockSpec((None,) + a.shape[1:], lambda i: (l, 0, 0))
-
+    vm = pl.BlockSpec(memory_space=pltpu.VMEM)
     args = [o_own, o_head, x, gain, w_out, w_peer, wg, wu, wd]
-    specs = [anys] * 3 + [layer_row(gain, layer)] + [anys] * 5
+    specs = [anys] * 3 + [vm] + [anys] * 5
     outs = [jax.ShapeDtypeStruct((rows, width), bf)]
     if next_qkv is not None:
         again, wq, wk, wv, bq, bk, bv, cos_tab, sin_tab = next_qkv
         args += list(next_qkv)
-        specs += [layer_row(again, layer + 1)] + [anys] * 3 + [layer_row(b, layer + 1) for b in (bq, bk, bv)] + [anys] * 2
+        specs += [vm] + [anys] * 3 + [vm] * 3 + [anys] * 2
         outs += [jax.ShapeDtypeStruct((rows, c), bf) for c in (wq.shape[2], HEAD_DIM, HEAD_DIM, 2 * HEAD_DIM)]
     return pl.pallas_call(
-        functools.partial(tail_kernel, layer=layer, tiles=tiles, chunks=chunks, head_rows=o_head.shape[0], with_qkv=next_qkv is not None),
-        grid=(1,),
+        functools.partial(tail_kernel, layer=layer, tile=tile, chunk=chunk, head_rows=o_head.shape[0], with_qkv=next_qkv is not None),
         in_specs=specs,
         out_specs=[anys] * len(outs),
         out_shape=outs,
         scratch_shapes=[
             pltpu.VMEM((2 * half, width), bf), pltpu.VMEM((rows, width), bf), pltpu.VMEM((rows, width), bf), pltpu.VMEM((rows, width), bf),
-            pltpu.VMEM((2, max(chunks), width), bf), pltpu.VMEM((max(chunks), width), jnp.float32),
+            pltpu.VMEM((2, chunk, width), bf), pltpu.VMEM((chunk, width), jnp.float32),
             pltpu.VMEM((width, cols), bf), pltpu.VMEM((width, cols), bf), pltpu.VMEM((cols, width), bf),
             dma((nt, 3)), dma((4,)), dma((nc,)), dma((2,)), dma((nc,)), dma((nc,)), dma((nc, 5)), dma((3 + 2 * nc,)),
         ],
@@ -451,12 +505,9 @@
         cos_half, sin_half = jnp.cos(angles), jnp.sin(angles)
         cos_tab = jnp.concatenate([cos_half, cos_half], axis=1)
         sin_tab = jnp.concatenate([-sin_half, sin_half], axis=1)
-        row = lambda a: a[:, None, :]
-        attn_gain, mlp_gain, b_query, b_key, b_value = (row(a) for a in (attn_gain, mlp_gain, b_query, b_key, b_value))
-
         qkv_args = (attn_gain, w_query, w_key, w_value, b_query, b_key, b_value, cos_tab, sin_tab)
         hidden, caches = x_in, []
-        q, k, v, kv = qkv(0, hidden, *qkv_args)
+        q, k, v, kv = qkv(hidden, *qkv_args)
         for layer, window_blocks in ((0, cp_size), (1, WINDOW // block_dev)):
             caches.append(k[:, None, :])
             caches.append(v[:, None, :])

time: 334 us -> 326 us (0.976); the launches traced: 331 us -> 326 us
  local copies, waits for them, and re-layouts: 20.1 us -> 7.25 us
  Pallas kernels: 306 us -> 315 us
    unnamed x39 -> x27, local copies, waits for them, and re-layouts: 15.6 us -> 7.25 us
    pallas_call x3, Pallas kernels: 182 us -> 188 us  [the longest x2 180 us: layer_tail(): pl.pallas_call(functools.partial(tail_kernel, layer=layer, tile=tile, chu...]
    broadcast_in_dim x5 -> x0, local copies, waits for them, and re-layouts: 4.52 us -> none  [local_step(): row = lambda a: a[:, None, :]]
where the time goes in v2:
time: 326 us
  Pallas kernels  315 us (97%)
  local copies, waits for them, and re-layouts  7.25 us (2%)
    pallas_call x2, Pallas kernels, layer_tail(): pl.pallas_call(functools.partial(tail_kernel, layer=layer, tile=tile, chu...  180 us
    pallas_call x2, Pallas kernels, attention(): pl.pallas_call(functools.partial(attn_kernel, layer=layer, bq=bq, window_...  127 us
    pallas_call x1, Pallas kernels, qkv(): pl.pallas_call(functools.partial(qkv_kernel, chunks=chunks), in_specs=[an...  8.66 us
    unnamed x27, local copies, waits for them, and re-layouts  7.25 us

profile of v2, /device:TPU:4, one launch (start us, length us, event | category | flops | bytes accessed | tf_op | source)
XLA Modules:
  0.0 326.2 jit_solution(7649764427383784533)
XLA Ops:
  0.6 0.0 copy-start.7
  0.6 0.0 copy-start.3
  0.7 0.0 copy-start.6
  0.7 0.0 copy-start.2
  0.7 0.0 copy-start.5
  0.7 0.0 copy-start.4
  0.7 0.8 convert_element_type.3
  1.5 1.9 fusion
  3.4 0.3 pad_maximum_fusion
  3.8 0.0 copy-start
  3.8 0.0 copy-start.1
  3.8 0.0 copy-done.7
  3.8 0.0 copy-done.3
  3.8 8.7 %qkv.1 = (bf16[1024,768]{1,0:T(8,128)(2,1)S(1)}, bf16[1024,128]{1,0:T(8,128)(2,1)}, bf16[1024,128]{1,0:T(8,128)(2,1)}, bf16[1024,256]{1,0:T(8,128)(2,1)S(1)}) custom-call(bf16[1024,1536]{1,0:T(8,128)(2,1)} %refs_2_.4, bf16[2,1536]{1,0:T(2,128)(2,1)S(1)} %copy-done.4, bf16[2,1536,768]{2,1,0:T(8,128)(2,1)} %refs_10_.1, bf16[2,1536,128]{2,1,0:T(8,128)(2,1)S(1)} %copy-done.2, ...), custom_call_target="tpu_custom_call" | custom-call | flops 3221225472 | bytes 9437184 | tf_op jit(solution)/shard_map/qkv/pallas_call | solution.py:89
  12.5 0.0 copy-start.8
  12.5 1.1 copy-done.8
  13.7 0.8 copy-done.9
  14.5 55.6 %attn.2 = (bf16[1024,768]{1,0:T(8,128)(2,1)}, bf16[512,768]{1,0:T(8,128)(2,1)}, bf16[768,1536]{1,0:T(8,128)(2,1)}) custom-call(bf16[1024,768]{1,0:T(8,128)(2,1)} %copy-done.8, bf16[1024,256]{1,0:T(8,128)(2,1)} %copy-done.9, bf16[2,768,1536]{2,1,0:T(8,128)(2,1)} %refs_4_.3), custom_call_target="tpu_custom_call" | custom-call | flops 12884901888 | bytes 4718592 | tf_op jit(solution)/shard_map/attn/pallas_call | solution.py:288
  70.1 90.6 %tail.2 = (bf16[1024,1536]{1,0:T(8,128)(2,1)}, bf16[1024,768]{1,0:T(8,128)(2,1)}, bf16[1024,128]{1,0:T(8,128)(2,1)}, bf16[1024,128]{1,0:T(8,128)(2,1)}, bf16[1024,256]{1,0:T(8,128)(2,1)}) custom-call(bf16[1024,768]{1,0:T(8,128)(2,1)} %get-tuple-element.22.refs_0_, bf16[512,768]{1,0:T(8,128)(2,1)} %get-tuple-element.23.refs_1_, bf16[1024,1536]{1,0:T(8,128)(2,1)} %refs_2_.4, ...), custom_call_target="tpu_custom_call" | custom-call | flops 42278584320 | bytes 41287680 | tf_op jit(solution)/shard_map/tail/pallas_call | solution.py:481
  160.8 71.2 %attn.3 = (bf16[1024,768]{1,0:T(8,128)(2,1)}, bf16[512,768]{1,0:T(8,128)(2,1)}, bf16[768,1536]{1,0:T(8,128)(2,1)}) custom-call(bf16[1024,768]{1,0:T(8,128)(2,1)} %get-tuple-element.25.refs_0_, bf16[1024,256]{1,0:T(8,128)(2,1)} %get-tuple-element.26.refs_1_, bf16[2,768,1536]{2,1,0:T(8,128)(2,1)} %refs_4_.3), custom_call_target="tpu_custom_call" | custom-call | flops 12884901888 | bytes 4718592 | tf_op jit(solution)/shard_map/attn/pallas_call | solution.py:288
  232.0 88.9 %tail.3 = bf16[1024,1536]{1,0:T(8,128)(2,1)} custom-call(bf16[1024,768]{1,0:T(8,128)(2,1)} %get-tuple-element.27.refs_0_, bf16[512,768]{1,0:T(8,128)(2,1)} %get-tuple-element.28.refs_1_, bf16[1024,1536]{1,0:T(8,128)(2,1)} %get-tuple-element.29.refs_2_, bf16[2,1536]{1,0:T(2,128)(2,1)} %refs_3_.3, bf16[2,768,1536]{2,1,0:T(8,128)(2,1)} %refs_4_.3, ...), custom_call_target="tpu_custom_call" | custom-call | flops 42278584320 | bytes 41287680 | tf_op jit(solution)/shard_map/tail/pallas_call | solution.py:481
  320.9 3.8 %copy.22 = bf16[1024,1536]{1,0:T(8,128)(2,1)} copy(bf16[1024,1536]{1,0:T(8,128)(2,1)} %tail.3) | data formatting | bytes 6291456
  324.8 0.7 copy.23
  325.5 0.7 copy.24
  (12 shorter events, 0.0 us)
Async XLA Ops:
  0.6 3.2 copy-start.7
  0.6 3.2 copy-start.3
  0.7 3.2 copy-start.6
  0.7 3.2 copy-start.2
  0.7 3.1 copy-start.5
  0.7 3.1 copy-start.4
  3.8 8.7 %copy-start = (f32[1024,128]{1,0:T(8,128)}, f32[1024,128]{1,0:T(8,128)S(1)}, u32[]{:S(2)}) copy-start(f32[1024,128]{1,0:T(8,128)S(1)} %get-tuple-element.38.cos_ref.refs_16_) | copy-start | bytes 1572868
  3.8 8.7 %copy-start.1 = (f32[1024,128]{1,0:T(8,128)}, f32[1024,128]{1,0:T(8,128)S(1)}, u32[]{:S(2)}) copy-start(f32[1024,128]{1,0:T(8,128)S(1)} %get-tuple-element.39.sin_ref.refs_17_) | copy-start | bytes 1572868
  12.5 1.1 copy-start.8
  13.7 0.8 copy-start.9
  320.9 3.8 %copy-start.11 = (bf16[1024,128]{1,0:T(8,128)(2,1)S(1)}, bf16[1024,128]{1,0:T(8,128)(2,1)}, u32[]{:S(2)}) copy-start(bf16[1024,128]{1,0:T(8,128)(2,1)} %get-tuple-element.33) | copy-start | bytes 786436
  320.9 4.5 %copy-start.10 = (bf16[1024,128]{1,0:T(8,128)(2,1)S(1)}, bf16[1024,128]{1,0:T(8,128)(2,1)}, u32[]{:S(2)}) copy-start(bf16[1024,128]{1,0:T(8,128)(2,1)} %get-tuple-element.34) | copy-start | bytes 786436
